TPU v7x, 256 devices: a whole 4x4x8 slice. The times are simulated.
256 devices in a mesh: gx: 16 (over z, core), gy: 16 (over x, y).
Axes of the slice: x: 4, y: 4, z: 8, core: 2. Of those that a mesh axis runs over, the one named last changes fastest.
Arguments:
- density: float32 [256, 256, 128], P('gx', 'gy'), may hold values from 0.05 to 40, as said below
Outputs:
- potential: float32 [256, 256, 128], P('gx', 'gy')
Inputs may be any that keep to these rules, and one draw needn't show every extreme that they name: `density`: densities are positive.
All inputs are finite; a program needn't handle non-finite values.
Results may differ from a plain program's by a relative error of at most 0.00014.
Values sent between devices are 32-bit elements; how exact they have to be, the bound alone decides.
A program may use at most 64 MiB of HBM per device.

v0:
```python
import jax
import jax.numpy as jnp
from jax import lax
from jax.sharding import Mesh
from jax.sharding import PartitionSpec as P

LEVELS = 4
NEWTON = 3
GX_GY = ("gx_0", "gx_1", "gy_0", "gy_1")
GX = ("gx_0", "gx_1")
GY = ("gy_0", "gy_1")


COUPLING = 0.1
FLOOR = 3.0


def extended(x, sides, width):
    for axis, dim in sides:
        peers, length = (lax.axis_size(axis), x.shape[dim])
        up = [(i, (i + 1) % peers) for i in range(peers)]
        down = [(j, i) for i, j in up]
        last = lax.slice_in_dim(x, length - width, length, axis=dim)
        leading = lax.slice_in_dim(x, 0, width, axis=dim)
        before = lax.ppermute(last, axis, up)
        after = lax.ppermute(leading, axis, down)
        x = jnp.concatenate([before, x, after], axis=dim)
    return x


def one_axis_at_a_time(x, axes):
    for axis in axes:
        x = lax.psum(x, axis)
    return x


def shifted(padded, off_x, off_y, off_z):
    size_x = padded.shape[0] - 2
    size_y = padded.shape[1] - 2
    size_z = padded.shape[2] - 2
    return padded[
        1 + off_x : 1 + off_x + size_x,
        1 + off_y : 1 + off_y + size_y,
        1 + off_z : 1 + off_z + size_z,
    ]


def hessian(padded, spacing_inv):
    center = shifted(padded, 0, 0, 0)
    pure_x = (shifted(padded, 1, 0, 0) + shifted(padded, -1, 0, 0) - 2.0 * center) * spacing_inv
    pure_y = (shifted(padded, 0, 1, 0) + shifted(padded, 0, -1, 0) - 2.0 * center) * spacing_inv
    pure_z = (shifted(padded, 0, 0, 1) + shifted(padded, 0, 0, -1) - 2.0 * center) * spacing_inv
    quarter = 0.25 * spacing_inv
    mixed_xy = (
        shifted(padded, 1, 1, 0)
        - shifted(padded, 1, -1, 0)
        - shifted(padded, -1, 1, 0)
        + shifted(padded, -1, -1, 0)
    ) * quarter
    mixed_xz = (
        shifted(padded, 1, 0, 1)
        - shifted(padded, 1, 0, -1)
        - shifted(padded, -1, 0, 1)
        + shifted(padded, -1, 0, -1)
    ) * quarter
    mixed_yz = (
        shifted(padded, 0, 1, 1)
        - shifted(padded, 0, 1, -1)
        - shifted(padded, 0, -1, 1)
        + shifted(padded, 0, -1, -1)
    ) * quarter
    return (pure_x, pure_y, pure_z, mixed_xy, mixed_xz, mixed_yz)


def nonlinear(padded, source):
    pure_x, pure_y, pure_z, mixed_xy, mixed_xz, mixed_yz = hessian(padded, 1.0)
    cubic = 2.0 * (
        pure_x * pure_y
        + pure_x * pure_z
        + pure_y * pure_z
        - mixed_xy * mixed_xy
        - mixed_xz * mixed_xz
        - mixed_yz * mixed_yz
    )
    return pure_x + pure_y + pure_z + COUPLING * cubic - source


def coefficients(padded, spacing_inv):
    pure_x, pure_y, pure_z, mixed_xy, mixed_xz, mixed_yz = hessian(padded, spacing_inv)
    stiff_x = 1.0 + 2.0 * COUPLING * (pure_y + pure_z)
    stiff_y = 1.0 + 2.0 * COUPLING * (pure_x + pure_z)
    stiff_z = 1.0 + 2.0 * COUPLING * (pure_x + pure_y)
    diagonal = jnp.maximum(2.0 * (stiff_x + stiff_y + stiff_z), FLOOR)
    relax = 1.0 / (spacing_inv * diagonal)
    return jnp.stack(
        [
            stiff_x,
            stiff_y,
            stiff_z,
            -4.0 * COUPLING * mixed_xy,
            -4.0 * COUPLING * mixed_xz,
            -4.0 * COUPLING * mixed_yz,
            relax,
        ]
    )


def jacobian(padded, weights, spacing_inv):
    parts = hessian(padded, spacing_inv)
    result = weights[0] * parts[0]
    for index in range(1, 6):
        result = result + weights[index] * parts[index]
    return result


def restrict(field):
    size_x, size_y, size_z = field.shape
    blocks = field.reshape(size_x // 2, 2, size_y // 2, 2, size_z // 2, 2)
    return jnp.sum(blocks, axis=(1, 3, 5)) * 0.125


def prolong(field):
    size_x, size_y, size_z = field.shape
    spread = jnp.broadcast_to(field[:, None, :, None, :, None], (size_x, 2, size_y, 2, size_z, 2))
    return spread.reshape(2 * size_x, 2 * size_y, 2 * size_z)


def wrap_depth(field):
    return jnp.concatenate([field[..., -1:], field, field[..., :1]], axis=-1)


def extend(field):
    return wrap_depth(extended(field, ((GX, 0), (GY, 1)), 1))


def checker(shape, first_x, first_y, first_z):
    index_x = first_x + jnp.arange(shape[0], dtype=jnp.int32)
    index_y = first_y + jnp.arange(shape[1], dtype=jnp.int32)
    index_z = first_z + jnp.arange(shape[2], dtype=jnp.int32)
    parity = (index_x[:, None, None] + index_y[None, :, None] + index_z[None, None, :]) % 2
    return (parity == 0).astype(jnp.float32)


def black_half(change, target, weights, red_mask, pad_field, spacing_inv):
    black_mask = 1.0 - red_mask
    return (
        change
        + black_mask * (jacobian(pad_field(change), weights, spacing_inv) - target) * weights[6]
    )


def first_sweep(target, weights, red_mask, pad_field, spacing_inv):
    change = -red_mask * target * weights[6]
    return black_half(change, target, weights, red_mask, pad_field, spacing_inv)


def full_sweep(change, target, weights, red_mask, pad_field, spacing_inv):
    change = (
        change
        + red_mask * (jacobian(pad_field(change), weights, spacing_inv) - target) * weights[6]
    )
    return black_half(change, target, weights, red_mask, pad_field, spacing_inv)


def edge_terms():
    return None


def start_sweep(target, context):
    weights, red_mask, spacing_inv, wide = context
    return first_sweep(target, weights, red_mask, extend, spacing_inv)


def more_sweep(change, target, context):
    weights, red_mask, spacing_inv, wide = context
    return full_sweep(change, target, weights, red_mask, extend, spacing_inv)


def cycle(coarse_level, target, weight_levels, mask_levels, wide_masks):
    spacing_inv = 0.25**coarse_level
    weights = weight_levels[coarse_level]
    red_mask = mask_levels[coarse_level]
    context = (weights, red_mask, spacing_inv, edge_terms())
    change = start_sweep(target, context)
    if coarse_level == LEVELS - 1:
        change = more_sweep(change, target, context)
        return change
    leftover = target - jacobian(extend(change), weights, spacing_inv)
    change = change + prolong(
        cycle(coarse_level + 1, restrict(leftover), weight_levels, mask_levels, wide_masks)
    )
    return more_sweep(change, target, context)


def per_device(density):
    cells_total = float(density.size * lax.axis_size(GX) * lax.axis_size(GY))
    mass_total = one_axis_at_a_time(jnp.sum(density), GX_GY)
    source = density / (mass_total / cells_total) - 1.0
    mask_levels = []
    wide_masks = []
    for coarse_level in range(LEVELS):
        shape = (
            density.shape[0] >> coarse_level,
            density.shape[1] >> coarse_level,
            density.shape[2] >> coarse_level,
        )
        start_x = lax.axis_index(GX) * shape[0]
        start_y = lax.axis_index(GY) * shape[1]
        mask_levels.append(checker(shape, start_x, start_y, 0))
        wide_shape = (shape[0] + 2, shape[1] + 2, shape[2] + 2)
        wide_masks.append(checker(wide_shape, start_x - 1, start_y - 1, -1))

    def newton_turn(newton_step, potential):
        padded_levels = []
        coarse = potential
        for coarse_level in range(LEVELS):
            if coarse_level > 0:
                coarse = restrict(coarse)
            padded_levels.append(extend(coarse))
        weight_levels = [
            coefficients(padded_levels[coarse_level], 0.25**coarse_level)
            for coarse_level in range(LEVELS)
        ]
        target = -nonlinear(padded_levels[0], source)
        return potential + cycle(0, target, weight_levels, mask_levels, wide_masks)

    return lax.fori_loop(0, NEWTON, newton_turn, jnp.zeros_like(density))


def solution(mesh):
    torus = Mesh(mesh.devices.reshape(8, 2, 4, 4), ("gx_0", "gx_1", "gy_0", "gy_1"))
    placed = (P(GX, GY, None),)
    return jax.shard_map(
        per_device, mesh=torus, in_specs=placed, out_specs=P(GX, GY, None), check_vma=False
    )
```

profile of v0, /device:TPU:1, one launch (start us, length us, event | category | flops | bytes accessed | tf_op | source)
XLA Modules:
  0.0 815.9 jit_solution(15661478614758730707)
XLA Ops:
  1.6 18.0 %psum.28 = f32[]{:T(128)} all-reduce(f32[]{:T(128)} %reduce_sum.87), channel_id=1, replica_groups=mesh['gx_0'=8,'gx_1'=2,'gy_0'=4,'gy_1'=4] {'gx_0'}, use_global_device_ids=true, to_apply=%region_1.0 | all-reduce | flops 1 | bytes 8 | tf_op jit(solution)/shard_map/psum | solution.py:33
  19.6 7.0 psum.29
  26.6 9.1 %psum.30 = f32[]{:T(128)} all-reduce(f32[]{:T(128)} %psum.29), channel_id=1, replica_groups=mesh['gx_0'=8,'gx_1'=2,'gy_0'=4,'gy_1'=4] {'gy_0'}, use_global_device_ids=true, to_apply=%region_3.0 | all-reduce | flops 1 | bytes 8 | tf_op jit(solution)/shard_map/psum | solution.py:33
  35.7 9.4 %psum.31 = f32[]{:T(128)} all-reduce(f32[]{:T(128)} %psum.30), channel_id=1, replica_groups=mesh['gx_0'=8,'gx_1'=2,'gy_0'=4,'gy_1'=4] {'gy_1'}, use_global_device_ids=true, to_apply=%region_4.0 | all-reduce | flops 1 | bytes 8 | tf_op jit(solution)/shard_map/psum | solution.py:33
  47.0 767.8 %while.16 = (s32[]{:T(128)}, f32[16,16,128]{2,1,0:T(8,128)S(1)}, f32[16,16,128]{2,1,0:T(8,128)S(1)}, s32[16,16]{1,0:T(8,128)S(1)}, s32[8,8]{1,0:T(8,128)S(1)}, /...) while((s32[]{:T(128)}, f32[16,16,128]{2,1,0:T(8,128)S(1)}, ...), condition=%wide.region_12.13_spmd.clone.clone.clone, body=%wide.region_5.12_spmd.clone.clone.clone.sunk | while | flops 16104283 | bytes 31824424 | solution.py:227
  47.3 4.4 collective-permute-start
  51.7 9.8 %reshape.257 = f32[8,2,8,2,64,2]{5,4,3,2,1,0:T(8,128)} reshape(f32[16,16,128]{2,1,0:T(8,128)S(1)} %broadcast_select_fusion.2) | data formatting | bytes 262144 | tf_op jit(solution)/shard_map/while/body/eval_jaxpr/reshape | solution.py:118
  74.9 4.9 collective-permute-start.39
  86.9 5.5 collective-permute-start.4
  105.8 4.7 collective-permute-start.8
  119.1 9.8 %reshape.256 = f32[8,2,8,2,64,2]{5,4,3,2,1,0:T(8,128)} reshape(f32[16,16,128]{2,1,0:T(8,128)S(1)} %fusion.546) | data formatting | bytes 262144 | tf_op jit(solution)/shard_map/while/body/eval_jaxpr/reshape | solution.py:118
  133.1 4.3 collective-permute-start.16
  141.2 4.8 collective-permute-done.19
  146.5 4.6 collective-permute-start.20
  160.0 4.3 collective-permute-start.28
  171.7 4.2 collective-permute-start.32
  183.9 4.2 collective-permute-start.40
  195.5 4.2 collective-permute-start.44
  207.2 4.2 collective-permute-start.48
  230.7 4.2 collective-permute-start.56
  243.2 4.2 collective-permute-start.60
  255.0 4.3 collective-permute-start.64
  271.1 6.9 reshape.262
  278.0 4.3 collective-permute-start.68
  290.3 4.3 collective-permute-start.72
  303.2 4.3 collective-permute-start
  307.5 9.8 %reshape.257 = f32[8,2,8,2,64,2]{5,4,3,2,1,0:T(8,128)} reshape(f32[16,16,128]{2,1,0:T(8,128)S(1)} %broadcast_select_fusion.2) | data formatting | bytes 262144 | tf_op jit(solution)/shard_map/while/body/eval_jaxpr/reshape | solution.py:118
  330.7 4.9 collective-permute-start.39
  342.7 5.5 collective-permute-start.4
  361.6 4.7 collective-permute-start.8
  374.5 9.8 %reshape.256 = f32[8,2,8,2,64,2]{5,4,3,2,1,0:T(8,128)} reshape(f32[16,16,128]{2,1,0:T(8,128)S(1)} %fusion.546) | data formatting | bytes 262144 | tf_op jit(solution)/shard_map/while/body/eval_jaxpr/reshape | solution.py:118
  388.4 4.3 collective-permute-start.16
  396.6 4.8 collective-permute-done.19
  401.9 4.6 collective-permute-start.20
  415.4 4.3 collective-permute-start.28
  427.1 4.2 collective-permute-start.32
  439.3 4.2 collective-permute-start.40
  462.6 4.2 collective-permute-start.48
  486.1 4.2 collective-permute-start.56
  498.6 4.2 collective-permute-start.60
  510.5 4.3 collective-permute-start.64
  526.7 6.9 reshape.262
  533.6 4.3 collective-permute-start.68
  545.9 4.3 collective-permute-start.72
  558.5 4.3 collective-permute-start
  562.9 9.8 %reshape.257 = f32[8,2,8,2,64,2]{5,4,3,2,1,0:T(8,128)} reshape(f32[16,16,128]{2,1,0:T(8,128)S(1)} %broadcast_select_fusion.2) | data formatting | bytes 262144 | tf_op jit(solution)/shard_map/while/body/eval_jaxpr/reshape | solution.py:118
  586.1 4.9 collective-permute-start.39
  598.1 5.5 collective-permute-start.4
  617.0 4.7 collective-permute-start.8
  630.1 9.8 %reshape.256 = f32[8,2,8,2,64,2]{5,4,3,2,1,0:T(8,128)} reshape(f32[16,16,128]{2,1,0:T(8,128)S(1)} %fusion.546) | data formatting | bytes 262144 | tf_op jit(solution)/shard_map/while/body/eval_jaxpr/reshape | solution.py:118
  644.0 4.3 collective-permute-start.16
  652.2 4.8 collective-permute-done.19
  657.5 4.6 collective-permute-start.20
  671.0 4.3 collective-permute-start.28
  682.7 4.2 collective-permute-start.32
  694.9 4.2 collective-permute-start.40
  706.5 4.2 collective-permute-start.44
  730.0 4.2 collective-permute-start.52
  741.7 4.2 collective-permute-start.56
  754.2 4.2 collective-permute-start.60
  766.0 4.3 collective-permute-start.64
  782.1 6.9 reshape.262
  789.0 4.3 collective-permute-start.68
  801.3 4.3 collective-permute-start.72
  (890 shorter events, 464.4 us)
Async XLA Ops:
  47.3 27.6 %collective-permute-start = (f32[1,16,128]{2,1,0:T(8,128)S(1)}, f32[1,16,128]{2,1,0:T(8,128)S(1)}, u32[]{:S(2)}, u32[]{:S(2)}) collective-permute-start(f32[1,16,128]{2,1,0:T(8,128)S(1)} %get-tuple-element.774), channel_id=1, source_target_pairs={{16,0},{32,16},{48,32},{64,48},{80,64},{96,80},{112,96},{128,112},... | collective-permute-start | bytes 24584 | tf_op jit(solution)/shard_map/while/body/eval_jaxpr/ppermute | solution.py:26
  51.7 28.1 %collective-permute-start.1 = (f32[1,16,128]{2,1,0:T(8,128)S(1)}, f32[1,16,128]{2,1,0:T(8,128)S(1)}, u32[]{:S(2)}, u32[]{:S(2)}) collective-permute-start(f32[1,16,128]{2,1,0:T(8,128)S(1)} %get-tuple-element.775), channel_id=1, source_target_pairs={{0,16},{16,32},{32,48},{48,64},{64,80},{80,96},{96,112},{112,128},... | collective-permute-start | bytes 24584 | tf_op jit(solution)/shard_map/while/body/eval_jaxpr/ppermute | solution.py:25
  65.5 14.4 %collective-permute-start.12 = (f32[1,8,64]{2,1,0:T(8,128)S(1)}, f32[1,8,64]{2,1,0:T(8,128)S(1)}, u32[]{:S(2)}, u32[]{:S(2)}) collective-permute-start(f32[1,8,64]{2,1,0:T(8,128)S(1)} %get-tuple-element.814), channel_id=1, source_target_pairs={{16,0},{32,16},{48,32},{64,48},{80,64},{96,80},{112,96},{128,112},... | collective-permute-start | bytes 6152 | tf_op jit(solution)/shard_map/while/body/eval_jaxpr/ppermute | solution.py:26
  73.9 6.2 collective-permute-start.13
  74.9 89.3 %collective-permute-start.38 = (f32[4,1,16]{2,1,0:T(1,128)S(1)}, f32[4,1,16]{2,1,0:T(1,128)S(1)}, u32[]{:S(2)}, u32[]{:S(2)}) collective-permute-start(f32[4,1,16]{2,1,0:T(1,128)S(1)} %get-tuple-element.892), channel_id=1, source_target_pairs={{0,1},{1,2},{2,3},{3,4},{4,5},{5,6},{6,7},{7,8},{8,9},{9,10},{10,1... | collective-permute-start | bytes 776 | tf_op jit(solution)/shard_map/while/body/eval_jaxpr/ppermute | solution.py:25
  74.9 89.3 %collective-permute-start.39 = (f32[4,1,16]{2,1,0:T(1,128)S(1)}, f32[4,1,16]{2,1,0:T(1,128)S(1)}, u32[]{:S(2)}, u32[]{:S(2)}) collective-permute-start(f32[4,1,16]{2,1,0:T(1,128)S(1)} %get-tuple-element.893), channel_id=1, source_target_pairs={{1,0},{2,1},{3,2},{4,3},{5,4},{6,5},{7,6},{8,7},{9,8},{10,9},{11,1... | collective-permute-start | bytes 776 | tf_op jit(solution)/shard_map/while/body/eval_jaxpr/ppermute | solution.py:26
  79.8 57.6 %collective-permute-start.26 = (f32[6,1,32]{2,1,0:T(1,128)S(1)}, f32[6,1,32]{2,1,0:T(1,128)S(1)}, u32[]{:S(2)}, u32[]{:S(2)}) collective-permute-start(f32[6,1,32]{2,1,0:T(1,128)S(1)} %get-tuple-element.854), channel_id=1, source_target_pairs={{1,0},{2,1},{3,2},{4,3},{5,4},{6,5},{7,6},{8,7},{9,8},{10,9},{11,1... | collective-permute-start | bytes 2312 | tf_op jit(solution)/shard_map/while/body/eval_jaxpr/ppermute | solution.py:26
  80.0 5.9 collective-permute-start.3
  86.0 6.5 collective-permute-start.15
  86.9 8.8 %collective-permute-start.4 = (f32[1,16,128]{2,1,0:T(8,128)S(1)}, f32[1,16,128]{2,1,0:T(8,128)S(1)}, u32[]{:S(2)}, u32[]{:S(2)}) collective-permute-start(f32[1,16,128]{2,1,0:T(8,128)S(1)} %get-tuple-element.787), channel_id=1, source_target_pairs={{16,0},{32,16},{48,32},{64,48},{80,64},{96,80},{112,96},{128,112},... | collective-permute-start | bytes 24584 | tf_op jit(solution)/shard_map/while/body/eval_jaxpr/ppermute | solution.py:26
  92.5 6.3 collective-permute-start.5
  112.4 5.9 collective-permute-start.11
  114.9 22.5 %collective-permute-start.27 = (f32[6,1,32]{2,1,0:T(1,128)S(1)}, f32[6,1,32]{2,1,0:T(1,128)S(1)}, u32[]{:S(2)}, u32[]{:S(2)}) collective-permute-start(f32[6,1,32]{2,1,0:T(1,128)S(1)} %get-tuple-element.855), channel_id=1, source_target_pairs={{0,1},{1,2},{2,3},{3,4},{4,5},{5,6},{6,7},{7,8},{8,9},{9,10},{10,1... | collective-permute-start | bytes 2312 | tf_op jit(solution)/shard_map/while/body/eval_jaxpr/ppermute | solution.py:25
  152.4 5.9 collective-permute-start.23
  165.5 5.8 collective-permute-start.31
  177.2 6.0 collective-permute-start.35
  224.5 5.8 collective-permute-start.55
  236.2 5.8 collective-permute-start.59
  248.7 5.9 collective-permute-start.63
  260.8 5.9 collective-permute-start.67
  283.6 5.9 collective-permute-start.71
  295.9 5.9 collective-permute-start.75
  303.2 27.6 %collective-permute-start = (f32[1,16,128]{2,1,0:T(8,128)S(1)}, f32[1,16,128]{2,1,0:T(8,128)S(1)}, u32[]{:S(2)}, u32[]{:S(2)}) collective-permute-start(f32[1,16,128]{2,1,0:T(8,128)S(1)} %get-tuple-element.774), channel_id=1, source_target_pairs={{16,0},{32,16},{48,32},{64,48},{80,64},{96,80},{112,96},{128,112},... | collective-permute-start | bytes 24584 | tf_op jit(solution)/shard_map/while/body/eval_jaxpr/ppermute | solution.py:26
  307.5 28.1 %collective-permute-start.1 = (f32[1,16,128]{2,1,0:T(8,128)S(1)}, f32[1,16,128]{2,1,0:T(8,128)S(1)}, u32[]{:S(2)}, u32[]{:S(2)}) collective-permute-start(f32[1,16,128]{2,1,0:T(8,128)S(1)} %get-tuple-element.775), channel_id=1, source_target_pairs={{0,16},{16,32},{32,48},{48,64},{64,80},{80,96},{96,112},{112,128},... | collective-permute-start | bytes 24584 | tf_op jit(solution)/shard_map/while/body/eval_jaxpr/ppermute | solution.py:25
  321.3 14.4 %collective-permute-start.12 = (f32[1,8,64]{2,1,0:T(8,128)S(1)}, f32[1,8,64]{2,1,0:T(8,128)S(1)}, u32[]{:S(2)}, u32[]{:S(2)}) collective-permute-start(f32[1,8,64]{2,1,0:T(8,128)S(1)} %get-tuple-element.814), channel_id=1, source_target_pairs={{16,0},{32,16},{48,32},{64,48},{80,64},{96,80},{112,96},{128,112},... | collective-permute-start | bytes 6152 | tf_op jit(solution)/shard_map/while/body/eval_jaxpr/ppermute | solution.py:26
  329.7 6.2 collective-permute-start.13
  330.7 88.9 %collective-permute-start.38 = (f32[4,1,16]{2,1,0:T(1,128)S(1)}, f32[4,1,16]{2,1,0:T(1,128)S(1)}, u32[]{:S(2)}, u32[]{:S(2)}) collective-permute-start(f32[4,1,16]{2,1,0:T(1,128)S(1)} %get-tuple-element.892), channel_id=1, source_target_pairs={{0,1},{1,2},{2,3},{3,4},{4,5},{5,6},{6,7},{7,8},{8,9},{9,10},{10,1... | collective-permute-start | bytes 776 | tf_op jit(solution)/shard_map/while/body/eval_jaxpr/ppermute | solution.py:25
  330.7 88.9 %collective-permute-start.39 = (f32[4,1,16]{2,1,0:T(1,128)S(1)}, f32[4,1,16]{2,1,0:T(1,128)S(1)}, u32[]{:S(2)}, u32[]{:S(2)}) collective-permute-start(f32[4,1,16]{2,1,0:T(1,128)S(1)} %get-tuple-element.893), channel_id=1, source_target_pairs={{1,0},{2,1},{3,2},{4,3},{5,4},{6,5},{7,6},{8,7},{9,8},{10,9},{11,1... | collective-permute-start | bytes 776 | tf_op jit(solution)/shard_map/while/body/eval_jaxpr/ppermute | solution.py:26
  335.6 57.1 %collective-permute-start.26 = (f32[6,1,32]{2,1,0:T(1,128)S(1)}, f32[6,1,32]{2,1,0:T(1,128)S(1)}, u32[]{:S(2)}, u32[]{:S(2)}) collective-permute-start(f32[6,1,32]{2,1,0:T(1,128)S(1)} %get-tuple-element.854), channel_id=1, source_target_pairs={{1,0},{2,1},{3,2},{4,3},{5,4},{6,5},{7,6},{8,7},{9,8},{10,9},{11,1... | collective-permute-start | bytes 2312 | tf_op jit(solution)/shard_map/while/body/eval_jaxpr/ppermute | solution.py:26
  335.8 5.9 collective-permute-start.3
  341.7 6.5 collective-permute-start.15
  342.7 8.8 %collective-permute-start.4 = (f32[1,16,128]{2,1,0:T(8,128)S(1)}, f32[1,16,128]{2,1,0:T(8,128)S(1)}, u32[]{:S(2)}, u32[]{:S(2)}) collective-permute-start(f32[1,16,128]{2,1,0:T(8,128)S(1)} %get-tuple-element.787), channel_id=1, source_target_pairs={{16,0},{32,16},{48,32},{64,48},{80,64},{96,80},{112,96},{128,112},... | collective-permute-start | bytes 24584 | tf_op jit(solution)/shard_map/while/body/eval_jaxpr/ppermute | solution.py:26
  348.3 6.3 collective-permute-start.5
  367.8 5.9 collective-permute-start.11
  370.3 22.5 %collective-permute-start.27 = (f32[6,1,32]{2,1,0:T(1,128)S(1)}, f32[6,1,32]{2,1,0:T(1,128)S(1)}, u32[]{:S(2)}, u32[]{:S(2)}) collective-permute-start(f32[6,1,32]{2,1,0:T(1,128)S(1)} %get-tuple-element.855), channel_id=1, source_target_pairs={{0,1},{1,2},{2,3},{3,4},{4,5},{5,6},{6,7},{7,8},{8,9},{9,10},{10,1... | collective-permute-start | bytes 2312 | tf_op jit(solution)/shard_map/while/body/eval_jaxpr/ppermute | solution.py:25
  407.7 5.9 collective-permute-start.23
  420.9 5.8 collective-permute-start.31
  432.6 6.1 collective-permute-start.35
  479.9 5.8 collective-permute-start.55
  491.6 5.8 collective-permute-start.59
  504.2 5.9 collective-permute-start.63
  516.4 5.9 collective-permute-start.67
  539.2 5.9 collective-permute-start.71
  551.5 5.9 collective-permute-start.75
  558.5 27.6 %collective-permute-start = (f32[1,16,128]{2,1,0:T(8,128)S(1)}, f32[1,16,128]{2,1,0:T(8,128)S(1)}, u32[]{:S(2)}, u32[]{:S(2)}) collective-permute-start(f32[1,16,128]{2,1,0:T(8,128)S(1)} %get-tuple-element.774), channel_id=1, source_target_pairs={{16,0},{32,16},{48,32},{64,48},{80,64},{96,80},{112,96},{128,112},... | collective-permute-start | bytes 24584 | tf_op jit(solution)/shard_map/while/body/eval_jaxpr/ppermute | solution.py:26
  562.8 28.1 %collective-permute-start.1 = (f32[1,16,128]{2,1,0:T(8,128)S(1)}, f32[1,16,128]{2,1,0:T(8,128)S(1)}, u32[]{:S(2)}, u32[]{:S(2)}) collective-permute-start(f32[1,16,128]{2,1,0:T(8,128)S(1)} %get-tuple-element.775), channel_id=1, source_target_pairs={{0,16},{16,32},{32,48},{48,64},{64,80},{80,96},{96,112},{112,128},... | collective-permute-start | bytes 24584 | tf_op jit(solution)/shard_map/while/body/eval_jaxpr/ppermute | solution.py:25
  576.7 14.4 %collective-permute-start.12 = (f32[1,8,64]{2,1,0:T(8,128)S(1)}, f32[1,8,64]{2,1,0:T(8,128)S(1)}, u32[]{:S(2)}, u32[]{:S(2)}) collective-permute-start(f32[1,8,64]{2,1,0:T(8,128)S(1)} %get-tuple-element.814), channel_id=1, source_target_pairs={{16,0},{32,16},{48,32},{64,48},{80,64},{96,80},{112,96},{128,112},... | collective-permute-start | bytes 6152 | tf_op jit(solution)/shard_map/while/body/eval_jaxpr/ppermute | solution.py:26
  585.0 6.2 collective-permute-start.13
  586.1 89.2 %collective-permute-start.38 = (f32[4,1,16]{2,1,0:T(1,128)S(1)}, f32[4,1,16]{2,1,0:T(1,128)S(1)}, u32[]{:S(2)}, u32[]{:S(2)}) collective-permute-start(f32[4,1,16]{2,1,0:T(1,128)S(1)} %get-tuple-element.892), channel_id=1, source_target_pairs={{0,1},{1,2},{2,3},{3,4},{4,5},{5,6},{6,7},{7,8},{8,9},{9,10},{10,1... | collective-permute-start | bytes 776 | tf_op jit(solution)/shard_map/while/body/eval_jaxpr/ppermute | solution.py:25
  586.1 89.1 %collective-permute-start.39 = (f32[4,1,16]{2,1,0:T(1,128)S(1)}, f32[4,1,16]{2,1,0:T(1,128)S(1)}, u32[]{:S(2)}, u32[]{:S(2)}) collective-permute-start(f32[4,1,16]{2,1,0:T(1,128)S(1)} %get-tuple-element.893), channel_id=1, source_target_pairs={{1,0},{2,1},{3,2},{4,3},{5,4},{6,5},{7,6},{8,7},{9,8},{10,9},{11,1... | collective-permute-start | bytes 776 | tf_op jit(solution)/shard_map/while/body/eval_jaxpr/ppermute | solution.py:26
  591.0 57.4 %collective-permute-start.26 = (f32[6,1,32]{2,1,0:T(1,128)S(1)}, f32[6,1,32]{2,1,0:T(1,128)S(1)}, u32[]{:S(2)}, u32[]{:S(2)}) collective-permute-start(f32[6,1,32]{2,1,0:T(1,128)S(1)} %get-tuple-element.854), channel_id=1, source_target_pairs={{1,0},{2,1},{3,2},{4,3},{5,4},{6,5},{7,6},{8,7},{9,8},{10,9},{11,1... | collective-permute-start | bytes 2312 | tf_op jit(solution)/shard_map/while/body/eval_jaxpr/ppermute | solution.py:26
  591.2 5.9 collective-permute-start.3
  597.1 6.5 collective-permute-start.15
  598.1 8.8 %collective-permute-start.4 = (f32[1,16,128]{2,1,0:T(8,128)S(1)}, f32[1,16,128]{2,1,0:T(8,128)S(1)}, u32[]{:S(2)}, u32[]{:S(2)}) collective-permute-start(f32[1,16,128]{2,1,0:T(8,128)S(1)} %get-tuple-element.787), channel_id=1, source_target_pairs={{16,0},{32,16},{48,32},{64,48},{80,64},{96,80},{112,96},{128,112},... | collective-permute-start | bytes 24584 | tf_op jit(solution)/shard_map/while/body/eval_jaxpr/ppermute | solution.py:26
  603.6 6.3 collective-permute-start.5
  623.4 5.9 collective-permute-start.11
  625.9 22.5 %collective-permute-start.27 = (f32[6,1,32]{2,1,0:T(1,128)S(1)}, f32[6,1,32]{2,1,0:T(1,128)S(1)}, u32[]{:S(2)}, u32[]{:S(2)}) collective-permute-start(f32[6,1,32]{2,1,0:T(1,128)S(1)} %get-tuple-element.855), channel_id=1, source_target_pairs={{0,1},{1,2},{2,3},{3,4},{4,5},{5,6},{6,7},{7,8},{8,9},{9,10},{10,1... | collective-permute-start | bytes 2312 | tf_op jit(solution)/shard_map/while/body/eval_jaxpr/ppermute | solution.py:25
  663.3 5.9 collective-permute-start.23
  688.2 6.0 collective-permute-start.35
  735.5 5.8 collective-permute-start.55
  759.7 5.9 collective-permute-start.63
  771.8 5.9 collective-permute-start.67
  794.5 5.9 collective-permute-start.71
  806.9 5.9 collective-permute-start.75
  (165 other events, 541.7 us)
where the time goes:
time: 819 us; the launch traced here: 816 us
  starting transfers between devices  338 us (41%)
  waiting for transfers between devices  270 us (33%)
  local copies, waits for them, and re-layouts  107 us (13%)
  other arithmetic  51 us (6%)
  blocking collectives  43.5 us (5%)
    ppermute x114, starting transfers between devices, extended(): after = lax.ppermute(leading, axis, down)  258 us
    ppermute x114, waiting for transfers between devices, extended(): before = lax.ppermute(last, axis, up)  180 us
    ppermute x114, waiting for transfers between devices, extended(): after = lax.ppermute(leading, axis, down)  90.6 us
    ppermute x114, starting transfers between devices, extended(): before = lax.ppermute(last, axis, up)  80.4 us
    reshape x12, local copies, waits for them, and re-layouts, restrict(): blocks = field.reshape(size_x // 2, 2, size_y // 2, 2, size_z // 2, 2)  62.2 us
    psum x4, blocking collectives, one_axis_at_a_time(): x = lax.psum(x, axis)  43.5 us
    reduce_sum x18, other arithmetic, restrict(): return jnp.sum(blocks, axis=(1, 3, 5)) * 0.125  25.8 us
    reshape x9, local copies, waits for them, and re-layouts, prolong(): return spread.reshape(2 * size_x, 2 * size_y, 2 * size_z)  23 us
  transfers between devices with their start and end apart: 228, of which 192 were waited for; matrix products, arithmetic and copies ran while one was open for 13% of the time, Pallas kernels for 0%

commit v1 on v0

v1 whole, which is shorter than its diff:
```python
import jax
import jax.numpy as jnp
from jax import lax
from jax.experimental import pallas as pl
from jax.experimental.pallas import tpu as pltpu
from jax.sharding import PartitionSpec as P

NEWTON = 3
COUPLING = 0.1
FLOOR = 3.0
RING = 16
LANES = 128
MESH = pl.DeviceIdType.MESH

HALO = 11
OWN = (12, 8, 12, 6)
SIZE_X = (40, 24, 28, 14)
SIZE_Y = (40, 24, 32, 16)
REACH = 3
BOX1 = [(i, j) for i in (-1, 0, 1) for j in (-1, 0, 1) if (i, j) != (0, 0)]
BOX3 = [
    (i, j)
    for i in range(-REACH, REACH + 1)
    for j in range(-REACH, REACH + 1)
    if (i, j) != (0, 0)
]
LINE_X = [(i, 0) for i in range(1, RING)]
LINE_Y = [(0, j) for j in range(1, RING)]


def rolled(value, shift, axis):
    return pltpu.roll(value, shift % value.shape[axis], axis)


def rows(start, stop, step, body):
    count = (stop - start) // step
    if count == 1:
        for j in range(step):
            body(start + j, j, (start + j) % 2)
    else:

        def chunk(i, carry):
            for j in range(step):
                body(start + i * step + j, j, (start + j) % 2)
            return carry

        lax.fori_loop(0, count, chunk, 0)
    for j in range(count * step, stop - start):
        body(start + j, j, (start + j) % 2)


def neighbours(below, centre, above, stride):
    yp, ym = rolled(centre, -1, 0), rolled(centre, 1, 0)
    zp, zm = rolled(centre, -stride, 1), rolled(centre, stride, 1)
    return above + below, yp + ym, zp + zm, yp - ym


def hessian(below, centre, above, stride):
    sum_x, sum_y, sum_z, diff_y = neighbours(below, centre, above, stride)
    twice = centre + centre
    diff_x = above - below
    mixed_xy = rolled(diff_x, -1, 0) - rolled(diff_x, 1, 0)
    mixed_xz = rolled(diff_x, -stride, 1) - rolled(diff_x, stride, 1)
    mixed_yz = rolled(diff_y, -stride, 1) - rolled(diff_y, stride, 1)
    return sum_x - twice, sum_y - twice, sum_z - twice, mixed_xy, mixed_xz, mixed_yz


def kernel(
    density, out, src, pot0, pot1, pot2, pot3,
    tgt0, tgt1, tgt2, tgt3, pre0, pre1, pre2, pre3,
    va0, va1, va2, va3, vb0, vb1, vb2, vb3,
    co0, co1, co2, co3, fold, packed_t, packed_u, got_t, got_u,
    mean_src, mean_x, mean_y, sends, recvs,
):
    gx, gy = lax.axis_index("gx"), lax.axis_index("gy")
    pot = (pot0, pot1, pot2, pot3)
    tgt = (tgt0, tgt1, tgt2, tgt3)
    pre = (pre0, pre1, pre2, pre3)
    va = (va0, va1, va2, va3)
    vb = (vb0, vb1, vb2, vb3)
    co = (co0, co1, co2, co3)

    def peer(dx, dy):
        return {"gx": lax.rem(gx + dx + RING, RING), "gy": lax.rem(gy + dy + RING, RING)}

    def send(src_ref, dst_ref, which, dx, dy):
        pltpu.make_async_remote_copy(
            src_ref=src_ref,
            dst_ref=dst_ref,
            send_sem=sends.at[which],
            recv_sem=recvs.at[which],
            device_id=peer(dx, dy),
            device_id_type=MESH,
        ).start()

    def finish(ref, sem):
        pltpu.make_async_copy(ref, ref, sem).wait()

    spans = {-1: (0, HALO), 0: (0, 16), 1: (16 - HALO, HALO)}
    lands = {-1: OWN[0] + 16, 0: OWN[0], 1: OWN[0] - HALO}

    def send_halo(src_ref, src_own, dst_ref, which):
        for dx, dy in BOX1:
            sx, nx = spans[dx]
            sy, ny = spans[dy]
            send(
                src_ref.at[pl.ds(src_own + sx, nx), pl.ds(src_own + sy, ny)],
                dst_ref.at[pl.ds(lands[dx], nx), pl.ds(lands[dy], ny)],
                which, dx, dy,
            )

    halo_bytes = co0.at[0, pl.ds(0, 33), pl.ds(0, 36)]

    def send_box(src_ref, dst_ref, which):
        for dx, dy in BOX3:
            at = pl.ds((REACH - dy) * 4, 4)
            if len(src_ref.shape) == 3:
                send(src_ref, dst_ref.at[REACH - dx, :, at], which, dx, dy)
            else:
                send(src_ref, dst_ref.at[REACH - dx, at], which, dx, dy)

    box_t_bytes = co0.at[0, pl.ds(0, 12), pl.ds(0, 32)]
    box_u_bytes = co0.at[0, pl.ds(0, 6), pl.ds(0, 32)]

    def lane_of(shape):
        return lax.broadcasted_iota(jnp.int32, shape, 1)

    def red_masks(level, size, first):
        shape = (size, LANES)
        parity = (
            lax.broadcasted_iota(jnp.int32, shape, 0) + first + (lane_of(shape) >> level)
        ) & 1
        return parity == 0, parity == 1

    def pair_z(value, level):
        stride = 1 << level
        low = ((lane_of(value.shape) >> level) & 1) == 0
        return value + jnp.where(low, rolled(value, -stride, 1), rolled(value, stride, 1))

    barrier = pltpu.get_barrier_semaphore()
    everyone = sorted(set(BOX3 + [(i - RING if i > 8 else i, 0) for i in range(1, RING)]
                          + [(0, j - RING if j > 8 else j) for j in range(1, RING)]))
    for dx, dy in everyone:
        pl.semaphore_signal(barrier, inc=1, device_id=peer(dx, dy), device_id_type=MESH)

    total = density[0]
    for x in range(1, 16):
        total = total + density[x]
    mean_src[0] = jnp.sum(total, axis=0, keepdims=True)
    mean_x[gx] = mean_src[0]

    def clear(x, j, parity):
        pot0[x] = jnp.zeros(pot0.shape[1:], jnp.float32)

    rows(0, SIZE_X[0], 4, clear)

    def clear2(x, j, parity):
        pot2[x] = jnp.zeros(pot2.shape[1:], jnp.float32)

    rows(0, SIZE_X[2], 4, clear2)
    pl.semaphore_wait(barrier, len(everyone))

    for dx, dy in LINE_X:
        send(mean_src.at[0], mean_x.at[gx], 0, dx, dy)
    send_halo(density, 0, src, 1)
    own = pl.ds(OWN[0], 16)

    def copy_own(x, j, parity):
        src[OWN[0] + x, own] = density[x]

    rows(0, 16, 4, copy_own)
    fifteen = mean_x.at[pl.ds(0, RING - 1)]
    finish(fifteen, recvs.at[0])
    row = mean_x[0]
    for i in range(1, RING):
        row = row + mean_x[i]
    mean_src[1] = row
    mean_y[gy] = row
    for dx, dy in LINE_Y:
        send(mean_src.at[1], mean_y.at[gy], 2, dx, dy)
    finish(fifteen, recvs.at[2])
    row = mean_y[0]
    for i in range(1, RING):
        row = row + mean_y[i]
    cells = RING * RING * 16 * 16 * LANES
    mean = jnp.sum(row, axis=1, keepdims=True) * (1.0 / cells)
    finish(halo_bytes, recvs.at[1])
    finish(fifteen, sends.at[0])
    finish(fifteen, sends.at[2])
    finish(halo_bytes, sends.at[1])

    def to_source(x, j, parity):
        src[x] = src[x] / mean - 1.0

    rows(1, 39, 2, to_source)

    def coefficients(level, start, stop, step, with_target=False):
        inv = 0.25**level
        field = pot[level]
        store = co[level]

        def body(x, j, parity):
            xx, yy, zz, xy, xz, yz = hessian(field[x - 1], field[x], field[x + 1], 1 << level)
            if level:
                xx, yy, zz = xx * inv, yy * inv, zz * inv
            quarter = 0.25 * inv
            stiff_x = 1.0 + 2.0 * COUPLING * (yy + zz)
            stiff_y = 1.0 + 2.0 * COUPLING * (xx + zz)
            stiff_z = 1.0 + 2.0 * COUPLING * (xx + yy)
            diagonal = jnp.maximum(2.0 * (stiff_x + stiff_y + stiff_z), FLOOR)
            relax = (1.0 / inv) / diagonal
            if level:
                store[0, x], store[1, x], store[2, x] = stiff_x * inv, stiff_y * inv, stiff_z * inv
            else:
                store[0, x], store[1, x], store[2, x] = stiff_x, stiff_y, stiff_z
            weight = -4.0 * COUPLING * quarter * quarter
            store[3, x], store[4, x], store[5, x] = xy * weight, xz * weight, yz * weight
            store[6, x] = relax
            if with_target:
                cubic = xx * yy + xx * zz + yy * zz - (xy * xy + xz * xz + yz * yz) * 0.0625
                target = src[x] - (xx + yy + zz + 2.0 * COUPLING * cubic)
                tgt[level][x] = target
                pre[level][x] = -target * relax

        rows(start, stop, step, body)

    def jacobian(level, field, x, ys):
        parts = hessian(field[x - 1, ys], field[x, ys], field[x + 1, ys], 1 << level)
        store = co[level]
        result = store[0, x, ys] * parts[0]
        for index in range(1, 6):
            result = result + store[index, x, ys] * parts[index]
        return result

    def whole(level):
        return pl.ds(0, SIZE_Y[level])

    def first_sweep(level, start, stop, step):
        masks = red_masks(level, SIZE_Y[level], 0)
        field, store = pre[level], co[level]

        def body(x, j, parity):
            centre = field[x]
            sum_x, sum_y, sum_z, _ = neighbours(field[x - 1], centre, field[x + 1], 1 << level)
            spread = store[0, x] * sum_x + store[1, x] * sum_y + store[2, x] * sum_z
            va[level][x] = jnp.where(masks[parity], centre, centre + spread * store[6, x])

        rows(start, stop, step, body)

    def half_sweep(level, colour, start, stop, step, ys, sink=None):
        masks = red_masks(level, ys.size, ys.start)
        from_ref, to_ref = (va, vb) if colour == 0 else (vb, va)
        from_ref, to_ref = from_ref[level], to_ref[level]

        def body(x, j, parity):
            old = from_ref[x, ys]
            change = (jacobian(level, from_ref, x, ys) - tgt[level][x, ys]) * co[level][6, x, ys]
            new = jnp.where(masks[(parity + colour) % 2], old + change, old)
            if sink is None:
                to_ref[x, ys] = new
            else:
                sink(x, new)

        rows(start, stop, step, body)

    def restricted(level, start, stop, pairs, first, count, sink):
        first_x, first_y = first

        def body(x, j, parity):
            fine = first_x + 2 * x
            acc = None
            for k in range(2):
                left = tgt[level][fine + k] - jacobian(level, va[level], fine + k, whole(level))
                acc = left if acc is None else acc + left
            slot = fold.at[j]
            slot[pl.ds(0, SIZE_Y[level]), :] = pair_z(acc, level)
            sink(x, 0.125 * (slot[pl.ds(first_y, count, 2), :] + slot[pl.ds(first_y + 1, count, 2), :]))

        rows(start, stop, pairs, body)

    def averaged(level, fine, first_y, count):
        field = pot[level]
        acc = None
        for k in range(2):
            for q in range(2):
                part = field[fine + k, pl.ds(first_y + q, count, 2), :]
                acc = part if acc is None else acc + part
        return 0.125 * pair_z(acc, level)

    def prolonged(level, start, stop, step, first_y, count, coarse_of, coarse_y):
        fine_ref, coarse_ref = va[level], va[level + 1]

        def body(x, j, parity):
            value = coarse_ref[x, pl.ds(coarse_y, count)]
            for k in range(2):
                for q in range(2):
                    at = (coarse_of(x) + k, pl.ds(first_y + q, count, 2), slice(None))
                    fine_ref[at] = fine_ref[at] + value

        rows(start, stop, step, body)

    quad = lane_of((4, LANES)) & 3

    def pack(values):
        return jnp.where(
            quad == 0, values[0], jnp.where(quad == 1, values[1], jnp.where(quad == 2, values[2], values[3]))
        )

    def unpack(read, write):
        place = lane_of((28, LANES)) & 3

        def body(g, j, parity):
            value = read(g)
            turned = {d: (value if d == 0 else rolled(value, -d, 1)) for d in range(-3, 4)}
            for i in range(4):
                piece = turned[i - 3]
                for k in (2, 1, 0):
                    piece = jnp.where(place == k, turned[i - k], piece)
                write(4 * g + i, piece)

        rows(0, 2 * REACH + 1, 1, body)

    def newton(step, carry):
        def coarse1(x, j, parity):
            pot1[x, pl.ds(2, 20)] = averaged(0, 2 * x - 4, 0, 20)

        rows(3, 21, 2, coarse1)
        coefficients(0, 2, 38, 2, with_target=True)
        coefficients(1, 4, 20, 2)
        coefficients(2, 12, 16, 2)
        first_sweep(0, 3, 37, 2)

        def to_level1(x, value):
            tgt1[4 + x, pl.ds(4, 16)] = value
            pre1[4 + x, pl.ds(4, 16)] = -value * co1[6, 4 + x, pl.ds(4, 16)]

        restricted(0, 0, 16, 2, (4, 4), 16, to_level1)
        first_sweep(1, 5, 19, 2)
        kept = []

        def to_level2(x, value):
            kept.append((value, -value * co2[6, 12 + x, pl.ds(12, 4)]))

        restricted(1, 0, 4, 4, (8, 8), 4, to_level2)
        packed_t[0] = pack([k[0] for k in kept])
        packed_t[1] = pack([k[1] for k in kept])
        send_box(packed_t, got_t, 3)
        for q in range(2):
            got_t[REACH, q, pl.ds(12, 4)] = packed_t[q]
        coefficients(2, 1, 12, 1)
        coefficients(2, 16, 27, 1)

        def coarse3(x, j, parity):
            pot3[x] = averaged(2, 2 * x, 0, 16)

        rows(0, 14, 2, coarse3)
        coefficients(3, 1, 13, 2)
        finish(box_t_bytes, recvs.at[3])

        def put(ref):
            def write(x, value):
                ref[x, pl.ds(0, 28)] = value

            return write

        unpack(lambda g: got_t[g, 0], put(tgt2))
        unpack(lambda g: got_t[g, 1], put(pre2))
        first_sweep(2, 1, 27, 2)

        def to_level3(x, value):
            tgt3[1 + x] = value
            pre3[1 + x] = -value * co3[6, 1 + x]

        restricted(2, 0, 12, 2, (2, 0), 16, to_level3)
        first_sweep(3, 2, 12, 2)
        half_sweep(3, 0, 3, 11, 2, whole(3))
        half_sweep(3, 1, 4, 10, 2, whole(3))
        prolonged(2, 4, 10, 2, 8, 6, lambda x: 2 * x, 4)
        half_sweep(2, 0, 9, 19, 2, pl.ds(8, 16))
        half_sweep(2, 1, 10, 18, 2, pl.ds(8, 16))
        prolonged(1, 10, 18, 2, 4, 8, lambda x: 2 * x - 16, 10)
        half_sweep(1, 0, 6, 18, 2, whole(1))
        half_sweep(1, 1, 7, 17, 2, whole(1))
        prolonged(0, 7, 17, 2, 10, 10, lambda x: 2 * x - 4, 7)
        half_sweep(0, 0, 11, 29, 2, pl.ds(8, 24))

        def add_own(x, new):
            pot0[x, own] = pot0[x, own] + new[4:20]

        half_sweep(0, 1, 12, 28, 2, pl.ds(8, 24), sink=add_own)
        finish(box_t_bytes, sends.at[3])

        @pl.when(step < NEWTON - 1)
        def _():
            send_halo(pot0, OWN[0], pot0, 1)

            def own1(x, j, parity):
                pot1[x, pl.ds(8, 8)] = averaged(0, 2 * x - 4, 12, 8)

            rows(8, 16, 4, own1)
            packed_u[...] = pack([averaged(1, 8 + 2 * x, 8, 4) for x in range(4)])
            send_box(packed_u, got_u, 4)
            got_u[REACH, pl.ds(12, 4)] = packed_u[...]
            finish(box_u_bytes, recvs.at[4])
            unpack(lambda g: got_u[g], put(pot2))
            finish(halo_bytes, recvs.at[1])
            finish(halo_bytes, sends.at[1])
            finish(box_u_bytes, sends.at[4])

        return carry

    lax.fori_loop(0, NEWTON, newton, 0)

    def result(x, j, parity):
        out[x] = pot0[OWN[0] + x, own]

    rows(0, 16, 4, result)


def per_device(density):
    def fields(count):
        return [
            pltpu.VMEM((SIZE_X[level], SIZE_Y[level], LANES), jnp.float32)
            for _ in range(count)
            for level in range(4)
        ]

    pots, tgts, pres, vas, vbs = (fields(1) for _ in range(5))
    cos = [pltpu.VMEM((7, SIZE_X[level], SIZE_Y[level], LANES), jnp.float32) for level in range(4)]
    return pl.pallas_call(
        kernel,
        out_shape=jax.ShapeDtypeStruct(density.shape, jnp.float32),
        in_specs=[pl.BlockSpec(memory_space=pltpu.VMEM)],
        out_specs=pl.BlockSpec(memory_space=pltpu.VMEM),
        scratch_shapes=[
            pltpu.VMEM((SIZE_X[0], SIZE_Y[0], LANES), jnp.float32),
            *pots, *tgts, *pres, *vas, *vbs, *cos,
            pltpu.VMEM((4, 40, LANES), jnp.float32),
            pltpu.VMEM((2, 4, LANES), jnp.float32),
            pltpu.VMEM((4, LANES), jnp.float32),
            pltpu.VMEM((7, 2, 28, LANES), jnp.float32),
            pltpu.VMEM((7, 28, LANES), jnp.float32),
            pltpu.VMEM((2, 1, LANES), jnp.float32),
            pltpu.VMEM((RING, 1, LANES), jnp.float32),
            pltpu.VMEM((RING, 1, LANES), jnp.float32),
            pltpu.SemaphoreType.DMA((5,)),
            pltpu.SemaphoreType.DMA((5,)),
        ],
        compiler_params=pltpu.CompilerParams(collective_id=0, has_side_effects=True),
    )(density)


def solution(mesh):
    return jax.shard_map(
        per_device,
        mesh=mesh,
        in_specs=(P("gx", "gy", None),),
        out_specs=P("gx", "gy", None),
        check_vma=False,
    )
```

time: 819 us -> 119 us (0.15)
  starting transfers between devices: 338 us -> 0 us
  waiting for transfers between devices: 270 us -> 0 us
  Pallas kernels: 0 us -> 118 us
  local copies, waits for them, and re-layouts: 107 us -> 1.57 us
  other arithmetic: 51 us -> 0 us
  blocking collectives: 43.5 us -> 0 us
    ppermute x228 -> x0, starting transfers between devices: 338 us -> none  [the longest x114 258 us: extended(): after = lax.ppermute(leading, axis, down)]
    ppermute x228 -> x0, waiting for transfers between devices: 270 us -> none  [the longest x114 180 us: extended(): before = lax.ppermute(last, axis, up)]
    pallas_call x0 -> x1, Pallas kernels: none -> 118 us  [per_device(): pl.pallas_call(kernel, out_shape=jax.ShapeDtypeStruct(density.shape, jnp....]
    reshape x21 -> x0, local copies, waits for them, and re-layouts: 85.2 us -> none  [the longest x12 62.2 us: restrict(): blocks = field.reshape(size_x // 2, 2, size_y // 2, 2, size_z // 2, 2)]
    psum x4 -> x0, blocking collectives: 43.5 us -> none  [one_axis_at_a_time(): x = lax.psum(x, axis)]
    reduce_sum x19 -> x0, other arithmetic: 27.4 us -> none  [the longest x18 25.8 us: restrict(): return jnp.sum(blocks, axis=(1, 3, 5)) * 0.125]
    broadcast_in_dim x9 -> x0, local copies, waits for them, and re-layouts: 12.8 us -> none  [prolong(): jnp.broadcast_to(field[:, None, :, None, :, None], (size_x, 2, size_y, 2,...]
    concatenate x216 -> x0, other arithmetic: 11.4 us -> none  [the longest x57 8.42 us: wrap_depth(): return jnp.concatenate([field[..., -1:], field, field[..., :1]], axis=-1)]
  transfers between devices with their start and end apart: 228 -> 0, of which waited for: 192 -> 0; matrix products, arithmetic and copies ran while one was open for 13% -> 0% of each run, Pallas kernels for 0% -> 0%
where the time goes in v1:
time: 119 us
  Pallas kernels  118 us (99%)
  local copies, waits for them, and re-layouts  1.57 us (1%)
    pallas_call x1, Pallas kernels, per_device(): pl.pallas_call(kernel, out_shape=jax.ShapeDtypeStruct(density.shape, jnp....  118 us

profile of v1, /device:TPU:1, one launch (start us, length us, event | category | flops | bytes accessed | tf_op | source)
XLA Modules:
  0.0 119.2 jit_solution(10680666953983086154)
XLA Ops:
  0.0 117.6 %shard_map.17 = f32[16,16,128]{2,1,0:T(8,128)} custom-call(f32[16,16,128]{2,1,0:T(8,128)} %density.1), custom_call_target="tpu_custom_call" | custom-call | tf_op jit(solution)/shard_map/pallas_call | solution.py:430
  117.6 1.6 %copy.3 = f32[16,16,128]{2,1,0:T(8,128)} copy(f32[16,16,128]{2,1,0:T(8,128)} %shard_map.17) | data formatting | bytes 262144

commit v2 on v1

--- a/solution.py
+++ b/solution.py
@@ -16,6 +16,8 @@
 OWN = (12, 8, 12, 6)
 SIZE_X = (40, 24, 28, 14)
 SIZE_Y = (40, 24, 32, 16)
+STEP = dict(coarse1=18, a0=12, a1=8, b0=34, c0=4, b1=14, a2=11, coarse3=14, a3=12, b2=26, c2=6, b3=10, e3=8, f3=6,
+            e2=10, f2=8, e1=12, f1=10, e0=18, f0=16, d2=6, d1=8, d0=10, un=7)
 REACH = 3
 BOX1 = [(i, j) for i in (-1, 0, 1) for j in (-1, 0, 1) if (i, j) != (0, 0)]
 BOX3 = [
@@ -38,6 +40,7 @@
         for j in range(step):
             body(start + j, j, (start + j) % 2)
     else:
+        assert step % 2 == 0 or step == 1
 
         def chunk(i, carry):
             for j in range(step):
@@ -318,24 +321,24 @@
                     piece = jnp.where(place == k, turned[i - k], piece)
                 write(4 * g + i, piece)
 
-        rows(0, 2 * REACH + 1, 1, body)
+        rows(0, 2 * REACH + 1, STEP['un'], body)
 
     def newton(step, carry):
         def coarse1(x, j, parity):
             pot1[x, pl.ds(2, 20)] = averaged(0, 2 * x - 4, 0, 20)
 
-        rows(3, 21, 2, coarse1)
-        coefficients(0, 2, 38, 2, with_target=True)
-        coefficients(1, 4, 20, 2)
-        coefficients(2, 12, 16, 2)
-        first_sweep(0, 3, 37, 2)
+        rows(3, 21, STEP['coarse1'], coarse1)
+        coefficients(0, 2, 38, STEP['a0'], with_target=True)
+        coefficients(1, 4, 20, STEP['a1'])
+        coefficients(2, 12, 16, 4)
+        first_sweep(0, 3, 37, STEP['b0'])
 
         def to_level1(x, value):
             tgt1[4 + x, pl.ds(4, 16)] = value
             pre1[4 + x, pl.ds(4, 16)] = -value * co1[6, 4 + x, pl.ds(4, 16)]
 
-        restricted(0, 0, 16, 2, (4, 4), 16, to_level1)
-        first_sweep(1, 5, 19, 2)
+        restricted(0, 0, 16, STEP['c0'], (4, 4), 16, to_level1)
+        first_sweep(1, 5, 19, STEP['b1'])
         kept = []
 
         def to_level2(x, value):
@@ -347,14 +350,14 @@
         send_box(packed_t, got_t, 3)
         for q in range(2):
             got_t[REACH, q, pl.ds(12, 4)] = packed_t[q]
-        coefficients(2, 1, 12, 1)
-        coefficients(2, 16, 27, 1)
+        coefficients(2, 1, 12, STEP['a2'])
+        coefficients(2, 16, 27, STEP['a2'])
 
         def coarse3(x, j, parity):
             pot3[x] = averaged(2, 2 * x, 0, 16)
 
-        rows(0, 14, 2, coarse3)
-        coefficients(3, 1, 13, 2)
+        rows(0, 14, STEP['coarse3'], coarse3)
+        coefficients(3, 1, 13, STEP['a3'])
         finish(box_t_bytes, recvs.at[3])
 
         def put(ref):
@@ -365,29 +368,29 @@
 
         unpack(lambda g: got_t[g, 0], put(tgt2))
         unpack(lambda g: got_t[g, 1], put(pre2))
-        first_sweep(2, 1, 27, 2)
+        first_sweep(2, 1, 27, STEP['b2'])
 
         def to_level3(x, value):
             tgt3[1 + x] = value
             pre3[1 + x] = -value * co3[6, 1 + x]
 
-        restricted(2, 0, 12, 2, (2, 0), 16, to_level3)
-        first_sweep(3, 2, 12, 2)
-        half_sweep(3, 0, 3, 11, 2, whole(3))
-        half_sweep(3, 1, 4, 10, 2, whole(3))
-        prolonged(2, 4, 10, 2, 8, 6, lambda x: 2 * x, 4)
-        half_sweep(2, 0, 9, 19, 2, pl.ds(8, 16))
-        half_sweep(2, 1, 10, 18, 2, pl.ds(8, 16))
-        prolonged(1, 10, 18, 2, 4, 8, lambda x: 2 * x - 16, 10)
-        half_sweep(1, 0, 6, 18, 2, whole(1))
-        half_sweep(1, 1, 7, 17, 2, whole(1))
-        prolonged(0, 7, 17, 2, 10, 10, lambda x: 2 * x - 4, 7)
-        half_sweep(0, 0, 11, 29, 2, pl.ds(8, 24))
+        restricted(2, 0, 12, STEP['c2'], (2, 0), 16, to_level3)
+        first_sweep(3, 2, 12, STEP['b3'])
+        half_sweep(3, 0, 3, 11, STEP['e3'], whole(3))
+        half_sweep(3, 1, 4, 10, STEP['f3'], whole(3))
+        prolonged(2, 4, 10, STEP['d2'], 8, 6, lambda x: 2 * x, 4)
+        half_sweep(2, 0, 9, 19, STEP['e2'], pl.ds(8, 16))
+        half_sweep(2, 1, 10, 18, STEP['f2'], pl.ds(8, 16))
+        prolonged(1, 10, 18, STEP['d1'], 4, 8, lambda x: 2 * x - 16, 10)
+        half_sweep(1, 0, 6, 18, STEP['e1'], whole(1))
+        half_sweep(1, 1, 7, 17, STEP['f1'], whole(1))
+        prolonged(0, 7, 17, STEP['d0'], 10, 10, lambda x: 2 * x - 4, 7)
+        half_sweep(0, 0, 11, 29, STEP['e0'], pl.ds(8, 24))
 
         def add_own(x, new):
             pot0[x, own] = pot0[x, own] + new[4:20]
 
-        half_sweep(0, 1, 12, 28, 2, pl.ds(8, 24), sink=add_own)
+        half_sweep(0, 1, 12, 28, STEP['f0'], pl.ds(8, 24), sink=add_own)
         finish(box_t_bytes, sends.at[3])
 
         @pl.when(step < NEWTON - 1)
@@ -435,7 +438,7 @@
         scratch_shapes=[
             pltpu.VMEM((SIZE_X[0], SIZE_Y[0], LANES), jnp.float32),
             *pots, *tgts, *pres, *vas, *vbs, *cos,
-            pltpu.VMEM((4, 40, LANES), jnp.float32),
+            pltpu.VMEM((16, 40, LANES), jnp.float32),
             pltpu.VMEM((2, 4, LANES), jnp.float32),
             pltpu.VMEM((4, LANES), jnp.float32),
             pltpu.VMEM((7, 2, 28, LANES), jnp.float32),

time: 119 us -> 90.5 us (0.76)
  Pallas kernels: 118 us -> 88.8 us
    pallas_call x1, Pallas kernels: 118 us -> 88.8 us  [per_device(): pl.pallas_call(kernel, out_shape=jax.ShapeDtypeStruct(density.shape, jnp....]
where the time goes in v2:
time: 90.5 us; the launch traced here: 90.4 us
  Pallas kernels  88.8 us (98%)
  local copies, waits for them, and re-layouts  1.57 us (2%)
    pallas_call x1, Pallas kernels, per_device(): pl.pallas_call(kernel, out_shape=jax.ShapeDtypeStruct(density.shape, jnp....  88.8 us

profile of v2, /device:TPU:1, one launch (start us, length us, event | category | flops | bytes accessed | tf_op | source)
XLA Modules:
  0.0 90.4 jit_solution(2149904988431699864)
XLA Ops:
  0.0 88.8 %shard_map.17 = f32[16,16,128]{2,1,0:T(8,128)} custom-call(f32[16,16,128]{2,1,0:T(8,128)} %density.1), custom_call_target="tpu_custom_call" | custom-call | tf_op jit(solution)/shard_map/pallas_call | solution.py:433
  88.9 1.6 %copy.3 = f32[16,16,128]{2,1,0:T(8,128)} copy(f32[16,16,128]{2,1,0:T(8,128)} %shard_map.17) | data formatting | bytes 262144

commit v3 on v2

--- a/solution.py
+++ b/solution.py
@@ -16,7 +16,7 @@
 OWN = (12, 8, 12, 6)
 SIZE_X = (40, 24, 28, 14)
 SIZE_Y = (40, 24, 32, 16)
-STEP = dict(coarse1=18, a0=12, a1=8, b0=34, c0=4, b1=14, a2=11, coarse3=14, a3=12, b2=26, c2=6, b3=10, e3=8, f3=6,
+STEP = dict(coarse1=18, a0=12, a1=8, b0=34, c0=4, b1=14, a2=26, coarse3=14, a3=12, b2=26, c2=6, b3=10, e3=8, f3=6,
             e2=10, f2=8, e1=12, f1=10, e0=18, f0=16, d2=6, d1=8, d0=10, un=7)
 REACH = 3
 BOX1 = [(i, j) for i in (-1, 0, 1) for j in (-1, 0, 1) if (i, j) != (0, 0)]
@@ -72,7 +72,7 @@
     density, out, src, pot0, pot1, pot2, pot3,
     tgt0, tgt1, tgt2, tgt3, pre0, pre1, pre2, pre3,
     va0, va1, va2, va3, vb0, vb1, vb2, vb3,
-    co0, co1, co2, co3, fold, packed_t, packed_u, got_t, got_u,
+    co0, co1, co2, co3, fold, packed_t, packed_u, got_0, got_t, got_u,
     mean_src, mean_x, mean_y, sends, recvs,
 ):
     gx, gy = lax.axis_index("gx"), lax.axis_index("gy")
@@ -102,17 +102,19 @@
     spans = {-1: (0, HALO), 0: (0, 16), 1: (16 - HALO, HALO)}
     lands = {-1: OWN[0] + 16, 0: OWN[0], 1: OWN[0] - HALO}
 
-    def send_halo(src_ref, src_own, dst_ref, which):
-        for dx, dy in BOX1:
+    def send_halo(src_ref, src_own, dst_ref, side, rest):
+        for dx, dy in [(0, 1), (0, -1)] + [o for o in BOX1 if o[0]]:
             sx, nx = spans[dx]
             sy, ny = spans[dy]
             send(
                 src_ref.at[pl.ds(src_own + sx, nx), pl.ds(src_own + sy, ny)],
                 dst_ref.at[pl.ds(lands[dx], nx), pl.ds(lands[dy], ny)],
-                which, dx, dy,
+                rest if dx else side, dx, dy,
             )
 
     halo_bytes = co0.at[0, pl.ds(0, 33), pl.ds(0, 36)]
+    side_bytes = co0.at[0, pl.ds(0, 11), pl.ds(0, 32)]
+    rest_bytes = co0.at[0, pl.ds(0, 38), pl.ds(0, 22)]
 
     def send_box(src_ref, dst_ref, which):
         for dx, dy in BOX3:
@@ -151,27 +153,17 @@
         total = total + density[x]
     mean_src[0] = jnp.sum(total, axis=0, keepdims=True)
     mean_x[gx] = mean_src[0]
-
-    def clear(x, j, parity):
-        pot0[x] = jnp.zeros(pot0.shape[1:], jnp.float32)
-
-    rows(0, SIZE_X[0], 4, clear)
-
-    def clear2(x, j, parity):
-        pot2[x] = jnp.zeros(pot2.shape[1:], jnp.float32)
-
-    rows(0, SIZE_X[2], 4, clear2)
     pl.semaphore_wait(barrier, len(everyone))
 
     for dx, dy in LINE_X:
         send(mean_src.at[0], mean_x.at[gx], 0, dx, dy)
-    send_halo(density, 0, src, 1)
+    send_halo(density, 0, src, 2, 2)
     own = pl.ds(OWN[0], 16)
 
     def copy_own(x, j, parity):
         src[OWN[0] + x, own] = density[x]
 
-    rows(0, 16, 4, copy_own)
+    rows(0, 16, 16, copy_own)
     fifteen = mean_x.at[pl.ds(0, RING - 1)]
     finish(fifteen, recvs.at[0])
     row = mean_x[0]
@@ -180,22 +172,8 @@
     mean_src[1] = row
     mean_y[gy] = row
     for dx, dy in LINE_Y:
-        send(mean_src.at[1], mean_y.at[gy], 2, dx, dy)
-    finish(fifteen, recvs.at[2])
-    row = mean_y[0]
-    for i in range(1, RING):
-        row = row + mean_y[i]
-    cells = RING * RING * 16 * 16 * LANES
-    mean = jnp.sum(row, axis=1, keepdims=True) * (1.0 / cells)
-    finish(halo_bytes, recvs.at[1])
-    finish(fifteen, sends.at[0])
-    finish(fifteen, sends.at[2])
-    finish(halo_bytes, sends.at[1])
-
-    def to_source(x, j, parity):
-        src[x] = src[x] / mean - 1.0
-
-    rows(1, 39, 2, to_source)
+        send(mean_src.at[1], mean_y.at[gy], 1, dx, dy)
+    finish(halo_bytes, recvs.at[2])
 
     def coefficients(level, start, stop, step, with_target=False):
         inv = 0.25**level
@@ -323,22 +301,171 @@
 
         rows(0, 2 * REACH + 1, STEP['un'], body)
 
+    def six(field, x, ys, level):
+        sum_x, sum_y, sum_z, _ = neighbours(field[x - 1, ys], field[x, ys], field[x + 1, ys], 1 << level)
+        return sum_x + sum_y + sum_z
+
+    def plain_first(level, start, stop, step):
+        masks = red_masks(level, SIZE_Y[level], 0)
+        relax = 4.0**level / 6.0
+        field = src if level == 0 else tgt[level]
+
+        def body(x, j, parity):
+            around = six(field, x, whole(level), level)
+            value = field[x]
+            va[level][x] = jnp.where(masks[parity], value, value + around * (1.0 / 6.0)) * -relax
+
+        rows(start, stop, step, body)
+
+    def plain_restricted(level, start, stop, pairs, first, count, sink):
+        first_x, first_y = first
+        field = src if level == 0 else tgt[level]
+        inv = 0.25**level
+
+        def body(x, j, parity):
+            fine = first_x + 2 * x
+            acc = None
+            for k in range(2):
+                centre = va[level][fine + k]
+                left = field[fine + k] - (six(va[level], fine + k, whole(level), level) - 6.0 * centre) * inv
+                acc = left if acc is None else acc + left
+            slot = fold.at[j]
+            slot[pl.ds(0, SIZE_Y[level]), :] = pair_z(acc, level)
+            sink(x, 0.125 * (slot[pl.ds(first_y, count, 2), :] + slot[pl.ds(first_y + 1, count, 2), :]))
+
+        rows(start, stop, pairs, body)
+
+    def plain_half(level, colour, start, stop, step, ys, sink=None):
+        masks = red_masks(level, ys.size, ys.start)
+        relax = 4.0**level / 6.0
+        from_ref, to_ref = (va, vb) if colour == 0 else (vb, va)
+        from_ref, to_ref = from_ref[level], to_ref[level]
+        field = src if level == 0 else tgt[level]
+
+        def body(x, j, parity):
+            moved = six(from_ref, x, ys, level) * (1.0 / 6.0) - field[x, ys] * relax
+            new = jnp.where(masks[(parity + colour) % 2], moved, from_ref[x, ys])
+            if sink is None:
+                to_ref[x, ys] = new
+            else:
+                sink(x, new)
+
+        rows(start, stop, step, body)
+
+    def put(ref):
+        def write(x, value):
+            ref[x, pl.ds(0, 28)] = value
+
+        return write
+
+    plain_first(0, 3, 37, STEP["b0"])
+
+    def raw1(x, value):
+        tgt1[4 + x, pl.ds(4, 16)] = value
+
+    plain_restricted(0, 0, 16, STEP["c0"], (4, 4), 16, raw1)
+    plain_first(1, 5, 19, STEP["b1"])
+    raw2 = []
+    plain_restricted(1, 0, 4, 4, (8, 8), 4, lambda x, value: raw2.append(value))
+    packed_t[0] = pack(raw2)
+    send_box(packed_t.at[0], got_0, 5)
+    got_0[REACH, pl.ds(12, 4)] = packed_t[0]
+    finish(fifteen, recvs.at[1])
+    row = mean_y[0]
+    for i in range(1, RING):
+        row = row + mean_y[i]
+    cells = RING * RING * 16 * 16 * LANES
+    scale = 1.0 / (jnp.sum(row, axis=1, keepdims=True) * (1.0 / cells))
+    finish(fifteen, sends.at[0])
+    finish(fifteen, sends.at[1])
+    finish(halo_bytes, sends.at[2])
+
+    def to_source(x, j, parity):
+        src[x] = src[x] * scale - 1.0
+
+    rows(1, 39, 2, to_source)
+
+    def to_values(level, start, stop, step):
+        masks = red_masks(level, SIZE_Y[level], 0)
+        relax = 4.0**level / 6.0
+
+        def body(x, j, parity):
+            va[level][x] = va[level][x] * scale + jnp.where(masks[parity], relax, 2.0 * relax)
+
+        rows(start, stop, step, body)
+
+    to_values(0, 10, 30, 4)
+    to_values(1, 5, 19, 2)
+
+    def to_target(x, j, parity):
+        tgt1[x] = tgt1[x] * scale - 1.0
+
+    rows(4, 20, 4, to_target)
+    finish(box_u_bytes, recvs.at[5])
+    unpack(lambda g: got_0[g] * scale - 1.0, put(tgt2))
+    plain_first(2, 1, 27, STEP["b2"])
+
+    def plain3(x, value):
+        tgt3[1 + x] = value
+
+    plain_restricted(2, 0, 12, STEP["c2"], (2, 0), 16, plain3)
+
+    def way_up(half, last):
+        prolonged(2, 4, 10, STEP["d2"], 8, 6, lambda x: 2 * x, 4)
+        half(2, 0, 9, 19, STEP["e2"], pl.ds(8, 16))
+        half(2, 1, 10, 18, STEP["f2"], pl.ds(8, 16))
+        prolonged(1, 10, 18, STEP["d1"], 4, 8, lambda x: 2 * x - 16, 10)
+        half(1, 0, 6, 18, STEP["e1"], whole(1))
+        half(1, 1, 7, 17, STEP["f1"], whole(1))
+        prolonged(0, 7, 17, STEP["d0"], 10, 10, lambda x: 2 * x - 4, 7)
+        half(0, 0, 11, 29, STEP["e0"], pl.ds(8, 24))
+        half(0, 1, 12, 28, STEP["f0"], pl.ds(8, 24), sink=last)
+
+    plain_first(3, 2, 12, STEP["b3"])
+    finish(box_u_bytes, sends.at[5])
+    plain_half(3, 0, 3, 11, STEP["e3"], whole(3))
+    plain_half(3, 1, 4, 10, STEP["f3"], whole(3))
+
+    def set_own(x, new):
+        pot0[x, own] = new[4:20]
+
+    way_up(plain_half, set_own)
+
     def newton(step, carry):
+        send_halo(pot0, OWN[0], pot0, 3, 4)
+
+        def own1(x, j, parity):
+            pot1[x, pl.ds(8, 8)] = averaged(0, 2 * x - 4, 12, 8)
+
+        rows(8, 16, 8, own1)
+        packed_u[...] = pack([averaged(1, 8 + 2 * x, 8, 4) for x in range(4)])
+        send_box(packed_u, got_u.at[step - 1], 5 + step)
+        got_u[step - 1, REACH, pl.ds(12, 4)] = packed_u[...]
+        finish(side_bytes, recvs.at[3])
+        coefficients(0, 13, 27, 14, with_target=True)
+        finish(rest_bytes, recvs.at[4])
+        coefficients(0, 2, 13, 11, with_target=True)
+        coefficients(0, 27, 38, 11, with_target=True)
+
         def coarse1(x, j, parity):
             pot1[x, pl.ds(2, 20)] = averaged(0, 2 * x - 4, 0, 20)
 
-        rows(3, 21, STEP['coarse1'], coarse1)
-        coefficients(0, 2, 38, STEP['a0'], with_target=True)
-        coefficients(1, 4, 20, STEP['a1'])
+        rows(3, 21, STEP["coarse1"], coarse1)
+        coefficients(1, 4, 20, STEP["a1"])
+
+        def coarse2(x, j, parity):
+            pot2[x, pl.ds(10, 8)] = averaged(1, 2 * x - 16, 4, 8)
+
+        rows(10, 18, 8, coarse2)
         coefficients(2, 12, 16, 4)
-        first_sweep(0, 3, 37, STEP['b0'])
+        first_sweep(0, 3, 37, STEP["b0"])
 
         def to_level1(x, value):
             tgt1[4 + x, pl.ds(4, 16)] = value
             pre1[4 + x, pl.ds(4, 16)] = -value * co1[6, 4 + x, pl.ds(4, 16)]
 
-        restricted(0, 0, 16, STEP['c0'], (4, 4), 16, to_level1)
-        first_sweep(1, 5, 19, STEP['b1'])
+        restricted(0, 0, 16, STEP["c0"], (4, 4), 16, to_level1)
+        first_sweep(1, 5, 19, STEP["b1"])
         kept = []
 
         def to_level2(x, value):
@@ -347,77 +474,48 @@
         restricted(1, 0, 4, 4, (8, 8), 4, to_level2)
         packed_t[0] = pack([k[0] for k in kept])
         packed_t[1] = pack([k[1] for k in kept])
-        send_box(packed_t, got_t, 3)
+        send_box(packed_t, got_t.at[step - 1], 7 + step)
         for q in range(2):
-            got_t[REACH, q, pl.ds(12, 4)] = packed_t[q]
-        coefficients(2, 1, 12, STEP['a2'])
-        coefficients(2, 16, 27, STEP['a2'])
+            got_t[step - 1, REACH, q, pl.ds(12, 4)] = packed_t[q]
+        finish(box_u_bytes, recvs.at[5 + step])
+        unpack(lambda g: got_u[step - 1, g], put(pot2))
+        coefficients(2, 1, 27, STEP["a2"])
 
         def coarse3(x, j, parity):
             pot3[x] = averaged(2, 2 * x, 0, 16)
 
-        rows(0, 14, STEP['coarse3'], coarse3)
-        coefficients(3, 1, 13, STEP['a3'])
-        finish(box_t_bytes, recvs.at[3])
-
-        def put(ref):
-            def write(x, value):
-                ref[x, pl.ds(0, 28)] = value
-
-            return write
-
-        unpack(lambda g: got_t[g, 0], put(tgt2))
-        unpack(lambda g: got_t[g, 1], put(pre2))
-        first_sweep(2, 1, 27, STEP['b2'])
+        rows(0, 14, STEP["coarse3"], coarse3)
+        coefficients(3, 1, 13, STEP["a3"])
+        finish(box_t_bytes, recvs.at[7 + step])
+        unpack(lambda g: got_t[step - 1, g, 0], put(tgt2))
+        unpack(lambda g: got_t[step - 1, g, 1], put(pre2))
+        first_sweep(2, 1, 27, STEP["b2"])
 
         def to_level3(x, value):
             tgt3[1 + x] = value
             pre3[1 + x] = -value * co3[6, 1 + x]
 
-        restricted(2, 0, 12, STEP['c2'], (2, 0), 16, to_level3)
-        first_sweep(3, 2, 12, STEP['b3'])
-        half_sweep(3, 0, 3, 11, STEP['e3'], whole(3))
-        half_sweep(3, 1, 4, 10, STEP['f3'], whole(3))
-        prolonged(2, 4, 10, STEP['d2'], 8, 6, lambda x: 2 * x, 4)
-        half_sweep(2, 0, 9, 19, STEP['e2'], pl.ds(8, 16))
-        half_sweep(2, 1, 10, 18, STEP['f2'], pl.ds(8, 16))
-        prolonged(1, 10, 18, STEP['d1'], 4, 8, lambda x: 2 * x - 16, 10)
-        half_sweep(1, 0, 6, 18, STEP['e1'], whole(1))
-        half_sweep(1, 1, 7, 17, STEP['f1'], whole(1))
-        prolonged(0, 7, 17, STEP['d0'], 10, 10, lambda x: 2 * x - 4, 7)
-        half_sweep(0, 0, 11, 29, STEP['e0'], pl.ds(8, 24))
+        restricted(2, 0, 12, STEP["c2"], (2, 0), 16, to_level3)
+        first_sweep(3, 2, 12, STEP["b3"])
+        half_sweep(3, 0, 3, 11, STEP["e3"], whole(3))
+        half_sweep(3, 1, 4, 10, STEP["f3"], whole(3))
+        finish(side_bytes, sends.at[3])
+        finish(rest_bytes, sends.at[4])
+        finish(box_u_bytes, sends.at[5 + step])
+        finish(box_t_bytes, sends.at[7 + step])
 
         def add_own(x, new):
             pot0[x, own] = pot0[x, own] + new[4:20]
 
-        half_sweep(0, 1, 12, 28, STEP['f0'], pl.ds(8, 24), sink=add_own)
-        finish(box_t_bytes, sends.at[3])
-
-        @pl.when(step < NEWTON - 1)
-        def _():
-            send_halo(pot0, OWN[0], pot0, 1)
-
-            def own1(x, j, parity):
-                pot1[x, pl.ds(8, 8)] = averaged(0, 2 * x - 4, 12, 8)
-
-            rows(8, 16, 4, own1)
-            packed_u[...] = pack([averaged(1, 8 + 2 * x, 8, 4) for x in range(4)])
-            send_box(packed_u, got_u, 4)
-            got_u[REACH, pl.ds(12, 4)] = packed_u[...]
-            finish(box_u_bytes, recvs.at[4])
-            unpack(lambda g: got_u[g], put(pot2))
-            finish(halo_bytes, recvs.at[1])
-            finish(halo_bytes, sends.at[1])
-            finish(box_u_bytes, sends.at[4])
-
+        way_up(half_sweep, add_own)
         return carry
 
-    lax.fori_loop(0, NEWTON, newton, 0)
+    lax.fori_loop(1, NEWTON, newton, 0)
 
     def result(x, j, parity):
         out[x] = pot0[OWN[0] + x, own]
 
-    rows(0, 16, 4, result)
+    rows(0, 16, 16, result)
 
 
 def per_device(density):
@@ -441,13 +539,14 @@
             pltpu.VMEM((16, 40, LANES), jnp.float32),
             pltpu.VMEM((2, 4, LANES), jnp.float32),
             pltpu.VMEM((4, LANES), jnp.float32),
-            pltpu.VMEM((7, 2, 28, LANES), jnp.float32),
             pltpu.VMEM((7, 28, LANES), jnp.float32),
+            pltpu.VMEM((2, 7, 2, 28, LANES), jnp.float32),
+            pltpu.VMEM((2, 7, 28, LANES), jnp.float32),
             pltpu.VMEM((2, 1, LANES), jnp.float32),
             pltpu.VMEM((RING, 1, LANES), jnp.float32),
             pltpu.VMEM((RING, 1, LANES), jnp.float32),
-            pltpu.SemaphoreType.DMA((5,)),
-            pltpu.SemaphoreType.DMA((5,)),
+            pltpu.SemaphoreType.DMA((10,)),
+            pltpu.SemaphoreType.DMA((10,)),
         ],
         compiler_params=pltpu.CompilerParams(collective_id=0, has_side_effects=True),
     )(density)

time: 90.5 us -> 80 us (0.88)
  Pallas kernels: 88.8 us -> 78.3 us
    pallas_call x1, Pallas kernels: 88.8 us -> 78.3 us  [per_device(): pl.pallas_call(kernel, out_shape=jax.ShapeDtypeStruct(density.shape, jnp....]
where the time goes in v3:
time: 80 us; the launch traced here: 79.9 us
  Pallas kernels  78.3 us (98%)
  local copies, waits for them, and re-layouts  1.57 us (2%)
    pallas_call x1, Pallas kernels, per_device(): pl.pallas_call(kernel, out_shape=jax.ShapeDtypeStruct(density.shape, jnp....  78.3 us

profile of v3, /device:TPU:1, one launch (start us, length us, event | category | flops | bytes accessed | tf_op | source)
XLA Modules:
  0.0 79.9 jit_solution(5340875183325676721)
XLA Ops:
  0.0 78.3 %shard_map.17 = f32[16,16,128]{2,1,0:T(8,128)} custom-call(f32[16,16,128]{2,1,0:T(8,128)} %density.1), custom_call_target="tpu_custom_call" | custom-call | tf_op jit(solution)/shard_map/pallas_call | solution.py:531
  78.4 1.6 %copy.3 = f32[16,16,128]{2,1,0:T(8,128)} copy(f32[16,16,128]{2,1,0:T(8,128)} %shard_map.17) | data formatting | bytes 262144

commit v4 on v3

--- a/solution.py
+++ b/solution.py
@@ -36,36 +36,70 @@
 
 def rows(start, stop, step, body):
     count = (stop - start) // step
+
+    def block(first, offsets):
+        cache = {}
+        for j in offsets:
+            body(first + j, j, (start + j) % 2, cache)
+
     if count == 1:
-        for j in range(step):
-            body(start + j, j, (start + j) % 2)
+        block(start, range(step))
     else:
         assert step % 2 == 0 or step == 1
 
         def chunk(i, carry):
-            for j in range(step):
-                body(start + i * step + j, j, (start + j) % 2)
+            block(start + i * step, range(step))
             return carry
 
         lax.fori_loop(0, count, chunk, 0)
-    for j in range(count * step, stop - start):
-        body(start + j, j, (start + j) % 2)
-
-
-def neighbours(below, centre, above, stride):
-    yp, ym = rolled(centre, -1, 0), rolled(centre, 1, 0)
-    zp, zm = rolled(centre, -stride, 1), rolled(centre, stride, 1)
-    return above + below, yp + ym, zp + zm, yp - ym
-
-
-def hessian(below, centre, above, stride):
-    sum_x, sum_y, sum_z, diff_y = neighbours(below, centre, above, stride)
+    if count * step < stop - start:
+        block(start, range(count * step, stop - start))
+
+
+def sum_y(value):
+    return rolled(value, -1, 0) + rolled(value, 1, 0)
+
+
+def diff_y(value):
+    return rolled(value, -1, 0) - rolled(value, 1, 0)
+
+
+def sum_z(value, stride):
+    return rolled(value, -stride, 1) + rolled(value, stride, 1)
+
+
+def turned(ref, x, j, ys, stride, cache):
+    if j not in cache:
+        value = ref[x, ys]
+        zp, zm = rolled(value, -stride, 1), rolled(value, stride, 1)
+        cache[j] = (value, zp + zm, zp - zm)
+    return cache[j]
+
+
+def hessian(ref, x, j, ys, stride, cache):
+    below, _, below_z = turned(ref, x - 1, j - 1, ys, stride, cache)
+    centre, along_z, centre_z = turned(ref, x, j, ys, stride, cache)
+    above, _, above_z = turned(ref, x + 1, j + 1, ys, stride, cache)
     twice = centre + centre
-    diff_x = above - below
-    mixed_xy = rolled(diff_x, -1, 0) - rolled(diff_x, 1, 0)
-    mixed_xz = rolled(diff_x, -stride, 1) - rolled(diff_x, stride, 1)
-    mixed_yz = rolled(diff_y, -stride, 1) - rolled(diff_y, stride, 1)
-    return sum_x - twice, sum_y - twice, sum_z - twice, mixed_xy, mixed_xz, mixed_yz
+    return (
+        above + below - twice,
+        sum_y(centre) - twice,
+        along_z - twice,
+        diff_y(above - below),
+        above_z - below_z,
+        diff_y(centre_z),
+    )
+
+
+def faces(ref, x, j, ys, stride, cache, keep):
+    if keep is None:
+        along_z = turned(ref, x, j, ys, stride, cache)[1]
+    elif j % 2 == 0:
+        cache[j] = sum_z(jnp.where(keep, ref[x, ys], ref[x + 1, ys]), stride)
+        along_z = cache[j]
+    else:
+        along_z = cache[j - 1]
+    return ref[x + 1, ys] + ref[x - 1, ys], sum_y(ref[x, ys]), along_z
 
 
 def kernel(
@@ -160,7 +194,7 @@
     send_halo(density, 0, src, 2, 2)
     own = pl.ds(OWN[0], 16)
 
-    def copy_own(x, j, parity):
+    def copy_own(x, j, parity, cache):
         src[OWN[0] + x, own] = density[x]
 
     rows(0, 16, 16, copy_own)
@@ -175,13 +209,16 @@
         send(mean_src.at[1], mean_y.at[gy], 1, dx, dy)
     finish(halo_bytes, recvs.at[2])
 
+    def whole(level):
+        return pl.ds(0, SIZE_Y[level])
+
     def coefficients(level, start, stop, step, with_target=False):
         inv = 0.25**level
         field = pot[level]
         store = co[level]
 
-        def body(x, j, parity):
-            xx, yy, zz, xy, xz, yz = hessian(field[x - 1], field[x], field[x + 1], 1 << level)
+        def body(x, j, parity, cache):
+            xx, yy, zz, xy, xz, yz = hessian(field, x, j, whole(level), 1 << level, cache)
             if level:
                 xx, yy, zz = xx * inv, yy * inv, zz * inv
             quarter = 0.25 * inv
@@ -205,25 +242,22 @@
 
         rows(start, stop, step, body)
 
-    def jacobian(level, field, x, ys):
-        parts = hessian(field[x - 1, ys], field[x, ys], field[x + 1, ys], 1 << level)
+    def jacobian(level, field, x, j, ys, cache):
+        parts = hessian(field, x, j, ys, 1 << level, cache)
         store = co[level]
         result = store[0, x, ys] * parts[0]
         for index in range(1, 6):
             result = result + store[index, x, ys] * parts[index]
         return result
 
-    def whole(level):
-        return pl.ds(0, SIZE_Y[level])
-
     def first_sweep(level, start, stop, step):
         masks = red_masks(level, SIZE_Y[level], 0)
         field, store = pre[level], co[level]
 
-        def body(x, j, parity):
+        def body(x, j, parity, cache):
             centre = field[x]
-            sum_x, sum_y, sum_z, _ = neighbours(field[x - 1], centre, field[x + 1], 1 << level)
-            spread = store[0, x] * sum_x + store[1, x] * sum_y + store[2, x] * sum_z
+            along = faces(field, x, j, whole(level), 1 << level, cache, masks[parity])
+            spread = store[0, x] * along[0] + store[1, x] * along[1] + store[2, x] * along[2]
             va[level][x] = jnp.where(masks[parity], centre, centre + spread * store[6, x])
 
         rows(start, stop, step, body)
@@ -233,9 +267,9 @@
         from_ref, to_ref = (va, vb) if colour == 0 else (vb, va)
         from_ref, to_ref = from_ref[level], to_ref[level]
 
-        def body(x, j, parity):
+        def body(x, j, parity, cache):
             old = from_ref[x, ys]
-            change = (jacobian(level, from_ref, x, ys) - tgt[level][x, ys]) * co[level][6, x, ys]
+            change = (jacobian(level, from_ref, x, j, ys, cache) - tgt[level][x, ys]) * co[level][6, x, ys]
             new = jnp.where(masks[(parity + colour) % 2], old + change, old)
             if sink is None:
                 to_ref[x, ys] = new
@@ -247,11 +281,11 @@
     def restricted(level, start, stop, pairs, first, count, sink):
         first_x, first_y = first
 
-        def body(x, j, parity):
+        def body(x, j, parity, cache):
             fine = first_x + 2 * x
             acc = None
             for k in range(2):
-                left = tgt[level][fine + k] - jacobian(level, va[level], fine + k, whole(level))
+                left = tgt[level][fine + k] - jacobian(level, va[level], fine + k, 2 * j + k, whole(level), cache)
                 acc = left if acc is None else acc + left
             slot = fold.at[j]
             slot[pl.ds(0, SIZE_Y[level]), :] = pair_z(acc, level)
@@ -271,7 +305,7 @@
     def prolonged(level, start, stop, step, first_y, count, coarse_of, coarse_y):
         fine_ref, coarse_ref = va[level], va[level + 1]
 
-        def body(x, j, parity):
+        def body(x, j, parity, cache):
             value = coarse_ref[x, pl.ds(coarse_y, count)]
             for k in range(2):
                 for q in range(2):
@@ -290,7 +324,7 @@
     def unpack(read, write):
         place = lane_of((28, LANES)) & 3
 
-        def body(g, j, parity):
+        def body(g, j, parity, cache):
             value = read(g)
             turned = {d: (value if d == 0 else rolled(value, -d, 1)) for d in range(-3, 4)}
             for i in range(4):
@@ -301,17 +335,17 @@
 
         rows(0, 2 * REACH + 1, STEP['un'], body)
 
-    def six(field, x, ys, level):
-        sum_x, sum_y, sum_z, _ = neighbours(field[x - 1, ys], field[x, ys], field[x + 1, ys], 1 << level)
-        return sum_x + sum_y + sum_z
+    def six(field, x, j, ys, level, cache, keep):
+        along = faces(field, x, j, ys, 1 << level, cache, keep)
+        return along[0] + along[1] + along[2]
 
     def plain_first(level, start, stop, step):
         masks = red_masks(level, SIZE_Y[level], 0)
         relax = 4.0**level / 6.0
         field = src if level == 0 else tgt[level]
 
-        def body(x, j, parity):
-            around = six(field, x, whole(level), level)
+        def body(x, j, parity, cache):
+            around = six(field, x, j, whole(level), level, cache, masks[parity])
             value = field[x]
             va[level][x] = jnp.where(masks[parity], value, value + around * (1.0 / 6.0)) * -relax
 
@@ -322,12 +356,13 @@
         field = src if level == 0 else tgt[level]
         inv = 0.25**level
 
-        def body(x, j, parity):
+        def body(x, j, parity, cache):
             fine = first_x + 2 * x
             acc = None
             for k in range(2):
                 centre = va[level][fine + k]
-                left = field[fine + k] - (six(va[level], fine + k, whole(level), level) - 6.0 * centre) * inv
+                around = six(va[level], fine + k, 2 * j + k, whole(level), level, cache, None)
+                left = field[fine + k] - (around - 6.0 * centre) * inv
                 acc = left if acc is None else acc + left
             slot = fold.at[j]
             slot[pl.ds(0, SIZE_Y[level]), :] = pair_z(acc, level)
@@ -342,9 +377,10 @@
         from_ref, to_ref = from_ref[level], to_ref[level]
         field = src if level == 0 else tgt[level]
 
-        def body(x, j, parity):
-            moved = six(from_ref, x, ys, level) * (1.0 / 6.0) - field[x, ys] * relax
-            new = jnp.where(masks[(parity + colour) % 2], moved, from_ref[x, ys])
+        def body(x, j, parity, cache):
+            other = masks[(parity + colour + 1) % 2]
+            around = six(from_ref, x, j, ys, level, cache, other)
+            new = jnp.where(other, from_ref[x, ys], around * (1.0 / 6.0) - field[x, ys] * relax)
             if sink is None:
                 to_ref[x, ys] = new
             else:
@@ -380,7 +416,7 @@
     finish(fifteen, sends.at[1])
     finish(halo_bytes, sends.at[2])
 
-    def to_source(x, j, parity):
+    def to_source(x, j, parity, cache):
         src[x] = src[x] * scale - 1.0
 
     rows(1, 39, 2, to_source)
@@ -389,7 +425,7 @@
         masks = red_masks(level, SIZE_Y[level], 0)
         relax = 4.0**level / 6.0
 
-        def body(x, j, parity):
+        def body(x, j, parity, cache):
             va[level][x] = va[level][x] * scale + jnp.where(masks[parity], relax, 2.0 * relax)
 
         rows(start, stop, step, body)
@@ -397,7 +433,7 @@
     to_values(0, 10, 30, 4)
     to_values(1, 5, 19, 2)
 
-    def to_target(x, j, parity):
+    def to_target(x, j, parity, cache):
         tgt1[x] = tgt1[x] * scale - 1.0
 
     rows(4, 20, 4, to_target)
@@ -434,7 +470,7 @@
     def newton(step, carry):
         send_halo(pot0, OWN[0], pot0, 3, 4)
 
-        def own1(x, j, parity):
+        def own1(x, j, parity, cache):
             pot1[x, pl.ds(8, 8)] = averaged(0, 2 * x - 4, 12, 8)
 
         rows(8, 16, 8, own1)
@@ -447,13 +483,13 @@
         coefficients(0, 2, 13, 11, with_target=True)
         coefficients(0, 27, 38, 11, with_target=True)
 
-        def coarse1(x, j, parity):
+        def coarse1(x, j, parity, cache):
             pot1[x, pl.ds(2, 20)] = averaged(0, 2 * x - 4, 0, 20)
 
         rows(3, 21, STEP["coarse1"], coarse1)
         coefficients(1, 4, 20, STEP["a1"])
 
-        def coarse2(x, j, parity):
+        def coarse2(x, j, parity, cache):
             pot2[x, pl.ds(10, 8)] = averaged(1, 2 * x - 16, 4, 8)
 
         rows(10, 18, 8, coarse2)
@@ -481,7 +517,7 @@
         unpack(lambda g: got_u[step - 1, g], put(pot2))
         coefficients(2, 1, 27, STEP["a2"])
 
-        def coarse3(x, j, parity):
+        def coarse3(x, j, parity, cache):
             pot3[x] = averaged(2, 2 * x, 0, 16)
 
         rows(0, 14, STEP["coarse3"], coarse3)
@@ -512,7 +548,7 @@
 
     lax.fori_loop(1, NEWTON, newton, 0)
 
-    def result(x, j, parity):
+    def result(x, j, parity, cache):
         out[x] = pot0[OWN[0] + x, own]
 
     rows(0, 16, 16, result)

time: 80 us -> 75.6 us (0.945)
  Pallas kernels: 78.3 us -> 73.9 us
    pallas_call x1, Pallas kernels: 78.3 us -> 73.9 us  [per_device(): pl.pallas_call(kernel, out_shape=jax.ShapeDtypeStruct(density.shape, jnp....]
where the time goes in v4:
time: 75.6 us; the launch traced here: 75.5 us
  Pallas kernels  73.9 us (98%)
  local copies, waits for them, and re-layouts  1.57 us (2%)
    pallas_call x1, Pallas kernels, per_device(): pl.pallas_call(kernel, out_shape=jax.ShapeDtypeStruct(density.shape, jnp....  73.9 us
    unnamed x1, local copies, waits for them, and re-layouts  1.57 us

profile of v4, /device:TPU:1, one launch (start us, length us, event | category | flops | bytes accessed | tf_op | source)
XLA Modules:
  0.0 75.5 jit_solution(1570886258262288482)
XLA Ops:
  0.0 73.9 %shard_map.17 = f32[16,16,128]{2,1,0:T(8,128)} custom-call(f32[16,16,128]{2,1,0:T(8,128)} %density.1), custom_call_target="tpu_custom_call" | custom-call | tf_op jit(solution)/shard_map/pallas_call | solution.py:567
  73.9 1.6 %copy.3 = f32[16,16,128]{2,1,0:T(8,128)} copy(f32[16,16,128]{2,1,0:T(8,128)} %shard_map.17) | data formatting | bytes 262144

commit v5 on v4

--- a/solution.py
+++ b/solution.py
@@ -26,6 +26,7 @@
     for j in range(-REACH, REACH + 1)
     if (i, j) != (0, 0)
 ]
+BOX3.sort(key=lambda o: -(abs(o[0]) + 2 * abs(o[1])))
 LINE_X = [(i, 0) for i in range(1, RING)]
 LINE_Y = [(0, j) for j in range(1, RING)]
 
@@ -107,7 +108,7 @@
     tgt0, tgt1, tgt2, tgt3, pre0, pre1, pre2, pre3,
     va0, va1, va2, va3, vb0, vb1, vb2, vb3,
     co0, co1, co2, co3, fold, packed_t, packed_u, got_0, got_t, got_u,
-    mean_src, mean_x, mean_y, sends, recvs,
+    mean_src, mean_x, mean_y, sends, recvs, local,
 ):
     gx, gy = lax.axis_index("gx"), lax.axis_index("gy")
     pot = (pot0, pot1, pot2, pot3)
@@ -133,20 +134,19 @@
     def finish(ref, sem):
         pltpu.make_async_copy(ref, ref, sem).wait()
 
-    spans = {-1: (0, HALO), 0: (0, 16), 1: (16 - HALO, HALO)}
-    lands = {-1: OWN[0] + 16, 0: OWN[0], 1: OWN[0] - HALO}
-
-    def send_halo(src_ref, src_own, dst_ref, side, rest):
-        for dx, dy in [(0, 1), (0, -1)] + [o for o in BOX1 if o[0]]:
+    def send_halo(ref, width, side, rest):
+        spans = {-1: (0, width), 0: (0, 16), 1: (16 - width, width)}
+        lands = {-1: OWN[0] + 16, 0: OWN[0], 1: OWN[0] - width}
+        for dx, dy in [(0, 1), (0, -1)] + [o for o in BOX1 if o[0] and o[1]] + [(1, 0), (-1, 0)]:
             sx, nx = spans[dx]
             sy, ny = spans[dy]
             send(
-                src_ref.at[pl.ds(src_own + sx, nx), pl.ds(src_own + sy, ny)],
-                dst_ref.at[pl.ds(lands[dx], nx), pl.ds(lands[dy], ny)],
+                ref.at[pl.ds(OWN[0] + sx, nx), pl.ds(OWN[0] + sy, ny)],
+                ref.at[pl.ds(lands[dx], nx), pl.ds(lands[dy], ny)],
                 rest if dx else side, dx, dy,
             )
 
-    halo_bytes = co0.at[0, pl.ds(0, 33), pl.ds(0, 36)]
+    halo_bytes = co0.at[0, pl.ds(0, 26), pl.ds(0, 40)]
     side_bytes = co0.at[0, pl.ds(0, 11), pl.ds(0, 32)]
     rest_bytes = co0.at[0, pl.ds(0, 38), pl.ds(0, 22)]
 
@@ -176,28 +176,26 @@
         low = ((lane_of(value.shape) >> level) & 1) == 0
         return value + jnp.where(low, rolled(value, -stride, 1), rolled(value, stride, 1))
 
+    fetch = pltpu.make_async_copy(density, src.at[pl.ds(OWN[0], 16), pl.ds(OWN[0], 16)], local.at[0])
+    fetch.start()
     barrier = pltpu.get_barrier_semaphore()
     everyone = sorted(set(BOX3 + [(i - RING if i > 8 else i, 0) for i in range(1, RING)]
                           + [(0, j - RING if j > 8 else j) for j in range(1, RING)]))
     for dx, dy in everyone:
         pl.semaphore_signal(barrier, inc=1, device_id=peer(dx, dy), device_id_type=MESH)
 
-    total = density[0]
+    own = pl.ds(OWN[0], 16)
+    fetch.wait()
+    total = src[OWN[0], own]
     for x in range(1, 16):
-        total = total + density[x]
+        total = total + src[OWN[0] + x, own]
     mean_src[0] = jnp.sum(total, axis=0, keepdims=True)
     mean_x[gx] = mean_src[0]
     pl.semaphore_wait(barrier, len(everyone))
 
+    send_halo(src, HALO - 1, 2, 2)
     for dx, dy in LINE_X:
         send(mean_src.at[0], mean_x.at[gx], 0, dx, dy)
-    send_halo(density, 0, src, 2, 2)
-    own = pl.ds(OWN[0], 16)
-
-    def copy_own(x, j, parity, cache):
-        src[OWN[0] + x, own] = density[x]
-
-    rows(0, 16, 16, copy_own)
     fifteen = mean_x.at[pl.ds(0, RING - 1)]
     finish(fifteen, recvs.at[0])
     row = mean_x[0]
@@ -468,7 +466,7 @@
     way_up(plain_half, set_own)
 
     def newton(step, carry):
-        send_halo(pot0, OWN[0], pot0, 3, 4)
+        send_halo(pot0, HALO, 3, 4)
 
         def own1(x, j, parity, cache):
             pot1[x, pl.ds(8, 8)] = averaged(0, 2 * x - 4, 12, 8)
@@ -567,7 +565,7 @@
     return pl.pallas_call(
         kernel,
         out_shape=jax.ShapeDtypeStruct(density.shape, jnp.float32),
-        in_specs=[pl.BlockSpec(memory_space=pltpu.VMEM)],
+        in_specs=[pl.BlockSpec(memory_space=pltpu.HBM)],
         out_specs=pl.BlockSpec(memory_space=pltpu.VMEM),
         scratch_shapes=[
             pltpu.VMEM((SIZE_X[0], SIZE_Y[0], LANES), jnp.float32),
@@ -583,8 +581,9 @@
             pltpu.VMEM((RING, 1, LANES), jnp.float32),
             pltpu.SemaphoreType.DMA((10,)),
             pltpu.SemaphoreType.DMA((10,)),
+            pltpu.SemaphoreType.DMA((1,)),
         ],
-        compiler_params=pltpu.CompilerParams(collective_id=0, has_side_effects=True),
+        compiler_params=pltpu.CompilerParams(collective_id=0, has_side_effects=True, vmem_limit_bytes=32 << 20),
     )(density)
 
 

time: 75.6 us -> 73.2 us (0.968)
  Pallas kernels: 73.9 us -> 71.6 us
    pallas_call x1, Pallas kernels: 73.9 us -> 71.6 us  [per_device(): pl.pallas_call(kernel, out_shape=jax.ShapeDtypeStruct(density.shape, jnp....]
    unnamed x1 -> x3, local copies, waits for them, and re-layouts: 1.57 us -> 1.56 us
where the time goes in v5:
time: 73.2 us
  Pallas kernels  71.6 us (98%)
  local copies, waits for them, and re-layouts  1.56 us (2%)
    pallas_call x1, Pallas kernels, per_device(): pl.pallas_call(kernel, out_shape=jax.ShapeDtypeStruct(density.shape, jnp....  71.6 us
    unnamed x3, local copies, waits for them, and re-layouts  1.56 us

profile of v5, /device:TPU:1, one launch (start us, length us, event | category | flops | bytes accessed | tf_op | source)
XLA Modules:
  0.0 73.2 jit_solution(5693166082289651826)
XLA Ops:
  0.0 0.0 copy-start
  0.0 0.9 %copy-done = f32[16,16,128]{2,1,0:T(8,128)S(1)} copy-done((f32[16,16,128]{2,1,0:T(8,128)S(1)}, f32[16,16,128]{2,1,0:T(8,128)}, u32[]{:S(2)}) %copy-start) | copy-done | bytes 131096
  0.9 71.6 %shard_map.17 = f32[16,16,128]{2,1,0:T(8,128)S(1)} custom-call(f32[16,16,128]{2,1,0:T(8,128)S(1)} %copy-done), custom_call_target="tpu_custom_call" | custom-call | tf_op jit(solution)/shard_map/pallas_call | solution.py:565
  72.5 0.7 copy.3
Async XLA Ops:
  0.0 0.9 %copy-start = (f32[16,16,128]{2,1,0:T(8,128)S(1)}, f32[16,16,128]{2,1,0:T(8,128)}, u32[]{:S(2)}) copy-start(f32[16,16,128]{2,1,0:T(8,128)} %density.1) | copy-start | bytes 393220

commit v6 on v5

--- a/solution.py
+++ b/solution.py
@@ -468,23 +468,20 @@
     def newton(step, carry):
         send_halo(pot0, HALO, 3, 4)
 
-        def own1(x, j, parity, cache):
-            pot1[x, pl.ds(8, 8)] = averaged(0, 2 * x - 4, 12, 8)
-
-        rows(8, 16, 8, own1)
+        finish(side_bytes, recvs.at[3])
+        coefficients(0, 13, 27, 14, with_target=True)
+        finish(rest_bytes, recvs.at[4])
+
+        def coarse1(x, j, parity, cache):
+            pot1[x, pl.ds(2, 20)] = averaged(0, 2 * x - 4, 0, 20)
+
+        rows(3, 21, STEP["coarse1"], coarse1)
         packed_u[...] = pack([averaged(1, 8 + 2 * x, 8, 4) for x in range(4)])
         send_box(packed_u, got_u.at[step - 1], 5 + step)
         got_u[step - 1, REACH, pl.ds(12, 4)] = packed_u[...]
-        finish(side_bytes, recvs.at[3])
-        coefficients(0, 13, 27, 14, with_target=True)
-        finish(rest_bytes, recvs.at[4])
         coefficients(0, 2, 13, 11, with_target=True)
         coefficients(0, 27, 38, 11, with_target=True)
 
-        def coarse1(x, j, parity, cache):
-            pot1[x, pl.ds(2, 20)] = averaged(0, 2 * x - 4, 0, 20)
-
-        rows(3, 21, STEP["coarse1"], coarse1)
         coefficients(1, 4, 20, STEP["a1"])
 
         def coarse2(x, j, parity, cache):

time: 73.2 us -> 72.5 us (level)
  Pallas kernels: 71.6 us -> 70.8 us
    pallas_call x1, Pallas kernels: 71.6 us -> 70.8 us  [per_device(): pl.pallas_call(kernel, out_shape=jax.ShapeDtypeStruct(density.shape, jnp....]
where the time goes in v6:
time: 72.5 us; the launch traced here: 72.4 us
  Pallas kernels  70.8 us (98%)
  local copies, waits for them, and re-layouts  1.56 us (2%)
    pallas_call x1, Pallas kernels, per_device(): pl.pallas_call(kernel, out_shape=jax.ShapeDtypeStruct(density.shape, jnp....  70.8 us
    unnamed x3, local copies, waits for them, and re-layouts  1.56 us

profile of v6, /device:TPU:1, one launch (start us, length us, event | category | flops | bytes accessed | tf_op | source)
XLA Modules:
  0.0 72.4 jit_solution(7252654881342361837)
XLA Ops:
  0.0 0.0 copy-start
  0.0 0.9 %copy-done = f32[16,16,128]{2,1,0:T(8,128)S(1)} copy-done((f32[16,16,128]{2,1,0:T(8,128)S(1)}, f32[16,16,128]{2,1,0:T(8,128)}, u32[]{:S(2)}) %copy-start) | copy-done | bytes 131096
  0.9 70.8 %shard_map.17 = f32[16,16,128]{2,1,0:T(8,128)S(1)} custom-call(f32[16,16,128]{2,1,0:T(8,128)S(1)} %copy-done), custom_call_target="tpu_custom_call" | custom-call | tf_op jit(solution)/shard_map/pallas_call | solution.py:562
  71.7 0.7 copy.3
Async XLA Ops:
  0.0 0.9 %copy-start = (f32[16,16,128]{2,1,0:T(8,128)S(1)}, f32[16,16,128]{2,1,0:T(8,128)}, u32[]{:S(2)}) copy-start(f32[16,16,128]{2,1,0:T(8,128)} %density.1) | copy-start | bytes 393220
